TPU v7x, 512 devices: a whole 4x8x8 slice. The times are simulated.
512 devices in a mesh: gx: 16 (over y, core), gy: 4 (over x), gz: 8 (over z).
Axes of the slice: x: 4, y: 8, z: 8, core: 2. Of those that a mesh axis runs over, the one named last changes fastest.
Arguments:
- fractions: float32 [3, 16, 8, 16, 128], P(None, 'gx', 'gy', 'gz'), may hold values from 0 to 1
- polarizability: float32 [16, 8, 16, 128], P('gx', 'gy', 'gz'), may hold values from 0.5 to 2
- occupancy: int32 [16, 8, 16, 128], P('gx', 'gy', 'gz'), may hold values 0 or 1
- pair_mask: int32 [16, 8, 16, 27], P('gx', 'gy', 'gz'), may hold values from 0 to 1, as said below
- perm_field: float32 [6, 16, 8, 16, 128], P(None, 'gx', 'gy', 'gz'), may hold values from -6 to 6
- history: float32 [6, 6, 16, 8, 16, 128], P(None, None, 'gx', 'gy', 'gz'), may hold values from -12 to 12
Outputs:
- induced: float32 [6, 16, 8, 16, 128], P(None, 'gx', 'gy', 'gz')
- change: float32 [], replicated
Inputs may be any that keep to these rules, and one draw needn't show every extreme that they name: pair_mask[t, k] equals pair_mask at tile t + offset(k) for the opposite offset 26 - k (periodic); pair_mask[t, 13] (the tile itself) is 1.
All inputs are finite; a program needn't handle non-finite values. No bound on the sum of `occupancy` on one device may be relied on, other than what follows from the above.
Results may differ from a plain program's by a relative error of at most 0.0003.
Values sent between devices are 32-bit elements; how exact they have to be, the bound alone decides.
A program may use at most 64 MiB of HBM per device.

v0:
```python
import functools

import jax
import jax.numpy as jnp
from jax import lax
from jax.sharding import Mesh
from jax.sharding import PartitionSpec as P

GX_GY_GZ = ("gx_0", "gx_1", "gy", "gz")
GX = ("gx_0", "gx_1")


CELL_EDGE = 10.0
SOFTENING = 0.3
THOLE_DAMP = 0.39
RELAXATION = 0.7


def with_halo(cells, sides, width):
    for axis, dim in sides:
        count = lax.axis_size(axis)
        head = lax.slice_in_dim(cells, 0, width, axis=dim)
        tail = lax.slice_in_dim(cells, cells.shape[dim] - width, cells.shape[dim], axis=dim)
        cells = jnp.concatenate(
            [
                lax.ppermute(tail, axis, [(i, (i + 1) % count) for i in range(count)]),
                cells,
                lax.ppermute(head, axis, [((i + 1) % count, i) for i in range(count)]),
            ],
            axis=dim,
        )
    return cells


def one_axis_at_a_time(shard, axes):
    return functools.reduce(lax.psum, axes, shard)


def pair_field(target, source, moment, offset_vec, itself, allowed):
    displace = [
        (offset_vec[axis_num] + source[axis_num][:, None, :] - target[axis_num][:, :, None])
        * CELL_EDGE
        for axis_num in range(3)
    ]
    dist_sq = (
        displace[0] * displace[0]
        + displace[1] * displace[1]
        + displace[2] * displace[2]
        + SOFTENING
    )
    inv_cube = lax.rsqrt(dist_sq) / dist_sq
    thole_arg = (
        dist_sq * jnp.sqrt(dist_sq) * lax.rsqrt(target[3][:, :, None] * source[3][:, None, :])
    )
    damping = jnp.exp(-THOLE_DAMP * thole_arg)
    lambda_three = 1.0 - damping
    lambda_five = 1.0 - (1.0 + THOLE_DAMP * thole_arg) * damping
    slots = target.shape[-1]
    self_pair = jnp.logical_and(itself, jnp.eye(slots, dtype=bool))
    weight = jnp.where(self_pair, 0.0, allowed[:, None, None])
    radial = 3.0 * lambda_five * inv_cube / dist_sq * weight
    direct = lambda_three * inv_cube * weight
    fields = []
    for which_set in range(moment.shape[0] // 3):
        parts = [moment[3 * which_set + axis_num][:, None, :] for axis_num in range(3)]
        project = displace[0] * parts[0] + displace[1] * parts[1] + displace[2] * parts[2]
        for axis_num in range(3):
            fields.append(
                jnp.sum(radial * project * displace[axis_num] - direct * parts[axis_num], axis=-1)
            )
    return jnp.stack(fields)


def slab_field(geometry_pad, moment_pad, allowed_slab, slab_index):
    width_y = geometry_pad.shape[2] - 2
    width_z = geometry_pad.shape[3] - 2
    slots = geometry_pad.shape[4]
    rows = moment_pad.shape[0]
    zero = jnp.zeros((), jnp.int32)
    one = jnp.ones((), jnp.int32)
    first_x = (jnp.asarray(slab_index) + 1).astype(jnp.int32)
    target = lax.dynamic_slice(
        geometry_pad, (zero, first_x, one, one, zero), (4, 1, width_y, width_z, slots)
    ).reshape(4, width_y * width_z, slots)

    def offset_step(offset, summed):
        offset = jnp.asarray(offset).astype(jnp.int32)
        along_x = offset // 9 - 1
        along_y = offset // 3 % 3 - 1
        along_z = offset % 3 - 1
        starts = (zero, first_x + along_x, one + along_y, one + along_z, zero)
        source = lax.dynamic_slice(geometry_pad, starts, (4, 1, width_y, width_z, slots)).reshape(
            4, width_y * width_z, slots
        )
        moment = lax.dynamic_slice(moment_pad, starts, (rows, 1, width_y, width_z, slots)).reshape(
            rows, width_y * width_z, slots
        )
        allowed = (
            lax.dynamic_index_in_dim(allowed_slab, offset, 2, keepdims=False)
            .reshape(-1)
            .astype(jnp.float32)
        )
        offset_vec = jnp.stack([along_x, along_y, along_z]).astype(jnp.float32)
        return summed + pair_field(target, source, moment, offset_vec, offset == 13, allowed)

    summed = lax.fori_loop(
        0, 27, offset_step, jnp.zeros((rows, width_y * width_z, slots), jnp.float32)
    )
    return summed.reshape(rows, width_y, width_z, slots)


def device_field(geometry_pad, moment_pad, pair_mask):
    slabs = [slab_field(geometry_pad, moment_pad, pair_mask[0], 0)]
    return jnp.stack(slabs, 1)


def share_dipoles(dipoles):
    return with_halo(dipoles, ((GX, 1), ("gy", 2), ("gz", 3)), 1)


def global_gram(local_gram):
    return one_axis_at_a_time(local_gram, GX_GY_GZ)


def fit_coefficients(gram_matrix):
    past_count = gram_matrix.shape[0] - 1
    gram_past = gram_matrix[:past_count, :past_count]
    gram_next = gram_matrix[:past_count, past_count]
    ridge_term = 0.001 * jnp.trace(gram_past) / past_count + 1.0
    factor = jnp.linalg.cholesky(gram_past + ridge_term * jnp.eye(past_count, dtype=jnp.float32))
    return jax.scipy.linalg.cho_solve((factor, True), gram_next)


def on_device(fractions, polarizability, occupancy, pair_mask, perm_field, history):
    filled = occupancy.astype(jnp.float32)
    geometry = jnp.concatenate([fractions, polarizability[None]], 0)
    masked = history * filled
    past_sets = masked.shape[0]
    flat_hist = masked.reshape(past_sets, -1)
    local_gram = jnp.dot(flat_hist, flat_hist.T, precision=lax.Precision.HIGHEST)
    scaled = RELAXATION * filled * polarizability
    later = masked[1:]
    stacked = jnp.concatenate([geometry, later.reshape((-1,) + later.shape[2:])], 0)
    ghosts = with_halo(stacked, ((GX, 1), ("gy", 2), ("gz", 3)), 1)
    coeffs = fit_coefficients(global_gram(local_gram))
    geometry_pad = ghosts[:4]
    later_pad = ghosts[4:].reshape((past_sets - 1, 6) + ghosts.shape[1:])
    predicted_pad = jnp.tensordot(coeffs, later_pad, axes=1, precision=lax.Precision.HIGHEST)
    predicted = predicted_pad[:, 1:-1, 1:-1, 1:-1, :]
    field_one = device_field(geometry_pad, predicted_pad, pair_mask)
    dipole_one = (1.0 - RELAXATION) * predicted + scaled * (perm_field + field_one)
    field_two = device_field(geometry_pad, share_dipoles(dipole_one), pair_mask)
    induced = (1.0 - RELAXATION) * dipole_one + scaled * (perm_field + field_two)
    update = induced - dipole_one
    totals = (
        one_axis_at_a_time(jnp.sum(update * update), GX_GY_GZ),
        one_axis_at_a_time(jnp.sum(induced * induced), GX_GY_GZ),
    )
    change = jnp.sqrt(totals[0] / (totals[1] + 1.0))
    return (induced, change)


def solution(mesh):
    split = Mesh(
        mesh.devices.reshape(8, 2, mesh.shape["gy"], mesh.shape["gz"]), ("gx_0", "gx_1", "gy", "gz")
    )
    placed = (
        P(None, GX, "gy", "gz", None),
        P(GX, "gy", "gz", None),
        P(GX, "gy", "gz", None),
        P(GX, "gy", "gz", None),
        P(None, GX, "gy", "gz", None),
        P(None, None, GX, "gy", "gz", None),
    )
    return jax.shard_map(
        on_device,
        mesh=split,
        in_specs=placed,
        out_specs=(P(None, GX, "gy", "gz", None), P()),
        check_vma=False,
    )
```

profile of v0, /device:TPU:1, one launch (start us, length us, event | category | flops | bytes accessed | tf_op | source)
XLA Modules:
  0.0 427.0 jit_solution(18372942800853096347)
XLA Ops:
  3.0 2.7 collective-permute-start
  5.7 4.2 collective-permute-start.1
  11.1 13.4 %psum.84 = f32[6,6]{0,1:T(8,128)S(1)} all-reduce(f32[6,6]{0,1:T(8,128)S(1)} %convolution_bitcast_fusion), channel_id=1, replica_groups=mesh['gx_0'=8,'gx_1'=2,'gy'=4,'gz'=8] {'gx_0'}, use_global_device_ids=true, to_apply=%region_0.0 | all-reduce | flops 36 | bytes 288 | tf_op jit(solution)/shard_map/psum | solution.py:36
  24.5 5.9 %psum.85 = f32[6,6]{0,1:T(8,128)S(1)} all-reduce(f32[6,6]{0,1:T(8,128)S(1)} %psum.84), channel_id=1, replica_groups=mesh['gx_0'=8,'gx_1'=2,'gy'=4,'gz'=8] {'gx_1'}, use_global_device_ids=true, to_apply=%region_1.0 | all-reduce | flops 36 | bytes 288 | tf_op jit(solution)/shard_map/psum | solution.py:36
  30.3 6.1 %psum.86 = f32[6,6]{0,1:T(8,128)S(1)} all-reduce(f32[6,6]{0,1:T(8,128)S(1)} %psum.85), channel_id=1, replica_groups=mesh['gx_0'=8,'gx_1'=2,'gy'=4,'gz'=8] {'gy'}, use_global_device_ids=true, to_apply=%region_2.0 | all-reduce | flops 36 | bytes 288 | tf_op jit(solution)/shard_map/psum | solution.py:36
  36.4 18.7 %psum.87 = f32[6,6]{0,1:T(8,128)S(1)} all-reduce(f32[6,6]{0,1:T(8,128)S(1)} %psum.86), channel_id=1, replica_groups=mesh['gx_0'=8,'gx_1'=2,'gy'=4,'gz'=8] {'gz'}, use_global_device_ids=true, to_apply=%region_3.0 | all-reduce | flops 36 | bytes 288 | tf_op jit(solution)/shard_map/psum | solution.py:36
  62.8 4.6 %collective-permute-start.3 = (f32[34,3,1,2,128]{4,3,2,1,0:T(2,128)S(1)}, f32[34,3,1,2,128]{4,3,2,1,0:T(2,128)S(1)}, u32[]{:S(2)}, u32[]{:S(2)}) collective-permute-start(f32[34,3,1,2,128]{4,3,2,1,0:T(2,128)S(1)} %get-tuple-element.668), channel_id=1, source_target_pairs={{8,0},{16,8},{24,16},{0,24},{9,1},{17,9},{25,17},{1,25},{10,2},{18... | collective-permute-start | bytes 313352 | tf_op jit(solution)/shard_map/ppermute | solution.py:28
  71.5 4.6 %collective-permute-start.5 = (f32[34,3,4,1,128]{4,3,2,1,0:T(1,128)S(1)}, f32[34,3,4,1,128]{4,3,2,1,0:T(1,128)S(1)}, u32[]{:S(2)}, u32[]{:S(2)}) collective-permute-start(f32[34,3,4,1,128]{4,3,2,1,0:T(1,128)S(1)} %get-tuple-element.666), channel_id=1, source_target_pairs={{1,0},{2,1},{3,2},{4,3},{5,4},{6,5},{7,6},{0,7},{9,8},{10,9},{11,1... | collective-permute-start | bytes 626696 | tf_op jit(solution)/shard_map/ppermute | solution.py:28
  81.9 133.7 %while.38 = (s32[]{:T(128)}, f32[6,4,128]{2,1,0:T(4,128)S(1)}, f32[4,3,4,4,128]{4,3,2,1,0:T(4,128)S(1)}, f32[4,4,128]{2,1,0:T(4,128)S(1)}, s32[2,2,27]{1,0,2:T(2...) while((s32[]{:T(128)}, f32[6,4,128]{2,1,0:T(4,128)S(1)}, ...), condition=%wide.region_14.15_spmd.clone, body=%wide.region_7.14_spmd.clone.sunk | while | flops 6200890 | bytes 262953 | solution.py:106
  87.6 1.9 constant_dynamic-slice_fusion.24
  92.6 1.9 constant_dynamic-slice_fusion.24
  112.4 1.9 constant_dynamic-slice_fusion.24
  117.4 1.9 constant_dynamic-slice_fusion.24
  132.2 1.9 constant_dynamic-slice_fusion.24
  137.2 1.9 constant_dynamic-slice_fusion.24
  215.6 8.8 %collective-permute-start.6 = (f32[6,1,2,2,128]{4,3,2,1,0:T(2,128)S(1)}, f32[6,1,2,2,128]{4,3,2,1,0:T(2,128)S(1)}, u32[]{:S(2)}, u32[]{:S(2)}) collective-permute-start(f32[6,1,2,2,128]{4,3,2,1,0:T(2,128)S(1)} %fusion.75), channel_id=1, source_target_pairs={{0,32},{32,64},{64,96},{96,128},{128,160},{160,192},{192,224},{224... | collective-permute-start | bytes 36872 | tf_op jit(solution)/shard_map/ppermute | solution.py:26
  225.3 2.6 collective-permute-done.7
  229.9 5.2 %collective-permute-start.9 = (f32[6,3,1,2,128]{4,3,2,1,0:T(2,128)S(1)}, f32[6,3,1,2,128]{4,3,2,1,0:T(2,128)S(1)}, u32[]{:S(2)}, u32[]{:S(2)}) collective-permute-start(f32[6,3,1,2,128]{4,3,2,1,0:T(2,128)S(1)} %get-tuple-element.672), channel_id=1, source_target_pairs={{8,0},{16,8},{24,16},{0,24},{9,1},{17,9},{25,17},{1,25},{10,2},{18... | collective-permute-start | bytes 55304 | tf_op jit(solution)/shard_map/ppermute | solution.py:28
  238.0 5.3 %collective-permute-start.11 = (f32[6,3,4,1,128]{4,3,2,1,0:T(1,128)S(1)}, f32[6,3,4,1,128]{4,3,2,1,0:T(1,128)S(1)}, u32[]{:S(2)}, u32[]{:S(2)}) collective-permute-start(f32[6,3,4,1,128]{4,3,2,1,0:T(1,128)S(1)} %get-tuple-element.670), channel_id=1, source_target_pairs={{1,0},{2,1},{3,2},{4,3},{5,4},{6,5},{7,6},{0,7},{9,8},{10,9},{11,1... | collective-permute-start | bytes 110600 | tf_op jit(solution)/shard_map/ppermute | solution.py:28
  244.5 133.6 %while.39 = (s32[]{:T(128)}, f32[6,4,128]{2,1,0:T(4,128)S(1)}, f32[4,3,4,4,128]{4,3,2,1,0:T(4,128)S(1)}, f32[4,4,128]{2,1,0:T(4,128)S(1)}, s32[2,2,27]{1,0,2:T(2...) while((s32[]{:T(128)}, f32[6,4,128]{2,1,0:T(4,128)S(1)}, ...), condition=%wide.region_22.23_spmd.clone, body=%wide.region_15.22_spmd.clone.sunk | while | flops 6200890 | bytes 262953 | solution.py:106
  379.3 14.4 %all-reduce.1 = (f32[]{:T(128)}, f32[]{:T(128)}) all-reduce(f32[]{:T(128)} %get-tuple-element.589, f32[]{:T(128)} %get-tuple-element.588), channel_id=1, replica_groups=mesh['gx_0'=8,'gx_1'=2,'gy'=4,'gz'=8] {'gx_0'}, use_global_device_ids=true, to_apply=%region_24.25 | all-reduce | flops 2 | bytes 16 | tf_op jit(solution)/shard_map/psum | solution.py:36
  393.7 6.2 %all-reduce.3 = (f32[]{:T(128)}, f32[]{:T(128)}) all-reduce(f32[]{:T(128)} %get-tuple-element.616, f32[]{:T(128)} %get-tuple-element.617), channel_id=1, replica_groups=mesh['gx_0'=8,'gx_1'=2,'gy'=4,'gz'=8] {'gx_1'}, use_global_device_ids=true, to_apply=%region_25.26 | all-reduce | flops 2 | bytes 16 | tf_op jit(solution)/shard_map/psum | solution.py:36
  400.0 9.9 %all-reduce.2 = (f32[]{:T(128)}, f32[]{:T(128)}) all-reduce(f32[]{:T(128)} %get-tuple-element.620, f32[]{:T(128)} %get-tuple-element.621), channel_id=1, replica_groups=mesh['gx_0'=8,'gx_1'=2,'gy'=4,'gz'=8] {'gy'}, use_global_device_ids=true, to_apply=%region_26.27 | all-reduce | flops 2 | bytes 16 | tf_op jit(solution)/shard_map/psum | solution.py:36
  409.9 14.8 %all-reduce = (f32[]{:T(128)}, f32[]{:T(128)}) all-reduce(f32[]{:T(128)} %get-tuple-element.618, f32[]{:T(128)} %get-tuple-element.619), channel_id=1, replica_groups=mesh['gx_0'=8,'gx_1'=2,'gy'=4,'gz'=8] {'gz'}, use_global_device_ids=true, to_apply=%region_27.28 | all-reduce | flops 2 | bytes 16 | tf_op jit(solution)/shard_map/psum | solution.py:36
  (1248 shorter events, 273.9 us)
Async XLA Ops:
  0.6 66.8 %copy-start.2 = (f32[1,2,2,128]{3,2,1,0:T(2,128)S(1)}, f32[1,2,2,128]{3,2,1,0:T(2,128)}, u32[]{:S(2)}) copy-start(f32[1,2,2,128]{3,2,1,0:T(2,128)} %param.11) | copy-start | bytes 6148
  0.6 66.8 %copy-start.1 = (f32[3,1,2,2,128]{4,3,2,1,0:T(2,128)S(1)}, f32[3,1,2,2,128]{4,3,2,1,0:T(2,128)}, u32[]{:S(2)}) copy-start(f32[3,1,2,2,128]{4,3,2,1,0:T(2,128)} %param.10) | copy-start | bytes 18436
  3.0 57.0 %collective-permute-start = (f32[34,1,2,2,128]{4,3,2,1,0:T(2,128)S(1)}, f32[34,1,2,2,128]{4,3,2,1,0:T(2,128)S(1)}, u32[]{:S(2)}, u32[]{:S(2)}) collective-permute-start(f32[34,1,2,2,128]{4,3,2,1,0:T(2,128)S(1)} %pad_maximum_fusion.5), channel_id=1, source_target_pairs={{0,32},{32,64},{64,96},{96,128},{128,160},{160,192},{192,224},{224... | collective-permute-start | bytes 208904 | tf_op jit(solution)/shard_map/ppermute | solution.py:26
  5.7 54.3 %collective-permute-start.1 = (f32[34,1,2,2,128]{4,3,2,1,0:T(2,128)S(1)}, f32[34,1,2,2,128]{4,3,2,1,0:T(2,128)S(1)}, u32[]{:S(2)}, u32[]{:S(2)}) collective-permute-start(f32[34,1,2,2,128]{4,3,2,1,0:T(2,128)S(1)} %pad_maximum_fusion.5), channel_id=1, source_target_pairs={{32,0},{64,32},{96,64},{128,96},{160,128},{192,160},{224,192},{256... | collective-permute-start | bytes 208904 | tf_op jit(solution)/shard_map/ppermute | solution.py:28
  60.9 6.6 %collective-permute-start.2 = (f32[34,3,1,2,128]{4,3,2,1,0:T(2,128)S(1)}, f32[34,3,1,2,128]{4,3,2,1,0:T(2,128)S(1)}, u32[]{:S(2)}, u32[]{:S(2)}) collective-permute-start(f32[34,3,1,2,128]{4,3,2,1,0:T(2,128)S(1)} %get-tuple-element.667), channel_id=1, source_target_pairs={{0,8},{8,16},{16,24},{24,0},{1,9},{9,17},{17,25},{25,1},{2,10},{10... | collective-permute-start | bytes 313352 | tf_op jit(solution)/shard_map/ppermute | solution.py:26
  62.8 6.3 %collective-permute-start.3 = (f32[34,3,1,2,128]{4,3,2,1,0:T(2,128)S(1)}, f32[34,3,1,2,128]{4,3,2,1,0:T(2,128)S(1)}, u32[]{:S(2)}, u32[]{:S(2)}) collective-permute-start(f32[34,3,1,2,128]{4,3,2,1,0:T(2,128)S(1)} %get-tuple-element.668), channel_id=1, source_target_pairs={{8,0},{16,8},{24,16},{0,24},{9,1},{17,9},{25,17},{1,25},{10,2},{18... | collective-permute-start | bytes 313352 | tf_op jit(solution)/shard_map/ppermute | solution.py:28
  67.5 8.7 %copy-start.4 = (s32[1,2,2,128]{3,2,1,0:T(2,128)S(1)}, s32[1,2,2,128]{3,2,1,0:T(2,128)}, u32[]{:S(2)}) copy-start(s32[1,2,2,128]{3,2,1,0:T(2,128)} %param.12) | copy-start | bytes 6148
  69.6 7.8 %collective-permute-start.4 = (f32[34,3,4,1,128]{4,3,2,1,0:T(1,128)S(1)}, f32[34,3,4,1,128]{4,3,2,1,0:T(1,128)S(1)}, u32[]{:S(2)}, u32[]{:S(2)}) collective-permute-start(f32[34,3,4,1,128]{4,3,2,1,0:T(1,128)S(1)} %get-tuple-element.665), channel_id=1, source_target_pairs={{0,1},{1,2},{2,3},{3,4},{4,5},{5,6},{6,7},{7,0},{8,9},{9,10},{10,1... | collective-permute-start | bytes 626696 | tf_op jit(solution)/shard_map/ppermute | solution.py:26
  71.5 7.3 %collective-permute-start.5 = (f32[34,3,4,1,128]{4,3,2,1,0:T(1,128)S(1)}, f32[34,3,4,1,128]{4,3,2,1,0:T(1,128)S(1)}, u32[]{:S(2)}, u32[]{:S(2)}) collective-permute-start(f32[34,3,4,1,128]{4,3,2,1,0:T(1,128)S(1)} %get-tuple-element.666), channel_id=1, source_target_pairs={{1,0},{2,1},{3,2},{4,3},{5,4},{6,5},{7,6},{0,7},{9,8},{10,9},{11,1... | collective-permute-start | bytes 626696 | tf_op jit(solution)/shard_map/ppermute | solution.py:28
  79.4 0.9 copy-start
  80.3 1.5 slice-start
  81.8 133.8 %copy-start.3 = (f32[6,1,2,2,128]{4,3,2,1,0:T(2,128)S(1)}, f32[6,1,2,2,128]{4,3,2,1,0:T(2,128)}, u32[]{:S(2)}) copy-start(f32[6,1,2,2,128]{4,3,2,1,0:T(2,128)} %param.14) | copy-start | bytes 36868
  215.6 9.7 %collective-permute-start.6 = (f32[6,1,2,2,128]{4,3,2,1,0:T(2,128)S(1)}, f32[6,1,2,2,128]{4,3,2,1,0:T(2,128)S(1)}, u32[]{:S(2)}, u32[]{:S(2)}) collective-permute-start(f32[6,1,2,2,128]{4,3,2,1,0:T(2,128)S(1)} %fusion.75), channel_id=1, source_target_pairs={{0,32},{32,64},{64,96},{96,128},{128,160},{160,192},{192,224},{224... | collective-permute-start | bytes 36872 | tf_op jit(solution)/shard_map/ppermute | solution.py:26
  224.5 3.4 collective-permute-start.7
  227.9 7.2 %collective-permute-start.8 = (f32[6,3,1,2,128]{4,3,2,1,0:T(2,128)S(1)}, f32[6,3,1,2,128]{4,3,2,1,0:T(2,128)S(1)}, u32[]{:S(2)}, u32[]{:S(2)}) collective-permute-start(f32[6,3,1,2,128]{4,3,2,1,0:T(2,128)S(1)} %get-tuple-element.671), channel_id=1, source_target_pairs={{0,8},{8,16},{16,24},{24,0},{1,9},{9,17},{17,25},{25,1},{2,10},{10... | collective-permute-start | bytes 55304 | tf_op jit(solution)/shard_map/ppermute | solution.py:26
  229.9 6.1 %collective-permute-start.9 = (f32[6,3,1,2,128]{4,3,2,1,0:T(2,128)S(1)}, f32[6,3,1,2,128]{4,3,2,1,0:T(2,128)S(1)}, u32[]{:S(2)}, u32[]{:S(2)}) collective-permute-start(f32[6,3,1,2,128]{4,3,2,1,0:T(2,128)S(1)} %get-tuple-element.672), channel_id=1, source_target_pairs={{8,0},{16,8},{24,16},{0,24},{9,1},{17,9},{25,17},{1,25},{10,2},{18... | collective-permute-start | bytes 55304 | tf_op jit(solution)/shard_map/ppermute | solution.py:28
  236.1 7.3 %collective-permute-start.10 = (f32[6,3,4,1,128]{4,3,2,1,0:T(1,128)S(1)}, f32[6,3,4,1,128]{4,3,2,1,0:T(1,128)S(1)}, u32[]{:S(2)}, u32[]{:S(2)}) collective-permute-start(f32[6,3,4,1,128]{4,3,2,1,0:T(1,128)S(1)} %get-tuple-element.669), channel_id=1, source_target_pairs={{0,1},{1,2},{2,3},{3,4},{4,5},{5,6},{6,7},{7,0},{8,9},{9,10},{10,1... | collective-permute-start | bytes 110600 | tf_op jit(solution)/shard_map/ppermute | solution.py:26
  238.0 6.4 %collective-permute-start.11 = (f32[6,3,4,1,128]{4,3,2,1,0:T(1,128)S(1)}, f32[6,3,4,1,128]{4,3,2,1,0:T(1,128)S(1)}, u32[]{:S(2)}, u32[]{:S(2)}) collective-permute-start(f32[6,3,4,1,128]{4,3,2,1,0:T(1,128)S(1)} %get-tuple-element.670), channel_id=1, source_target_pairs={{1,0},{2,1},{3,2},{4,3},{5,4},{6,5},{7,6},{0,7},{9,8},{10,9},{11,1... | collective-permute-start | bytes 110600 | tf_op jit(solution)/shard_map/ppermute | solution.py:28
where the time goes:
time: 433 us; the launch traced here: 427 us
  other arithmetic  223 us (52%)
  blocking collectives  89.3 us (21%)
  local copies, waits for them, and re-layouts  45.7 us (11%)
  starting transfers between devices  43.1 us (10%)
  loops' own time  10.2 us (2%)
  waiting for transfers between devices  9.63 us (2%)
    slice x54, other arithmetic, pair_field(): moment[3 * which_set + axis_num][:, None, :]  104 us
    reduce_sum x108, other arithmetic, pair_field(): jnp.sum(radial * project * displace[axis_num] - direct * parts[axis_num],...  102 us
    psum x8, blocking collectives, one_axis_at_a_time(): return functools.reduce(lax.psum, axes, shard)  89.3 us
    slice x54, local copies, waits for them, and re-layouts, pair_field(): offset_vec[axis_num] + source[axis_num][:, None, :]  36 us
    ppermute x6, starting transfers between devices, with_halo(): lax.ppermute(head, axis, [((i + 1) % count, i) for i in range(count)])  23.9 us
    ppermute x6, starting transfers between devices, with_halo(): lax.ppermute(tail, axis, [(i, (i + 1) % count) for i in range(count)])  19.2 us
    another operation x2, loops' own time, slab_field(): lax.fori_loop(0, 27, offset_step, jnp.zeros((rows, width_y * width_z, slo...  10.2 us
  transfers between devices with their start and end apart: 12, of which 8 were waited for; matrix products, arithmetic and copies ran while one was open for 1% of the time, Pallas kernels for 0%

commit v1 on v0

v1 whole, which is shorter than its diff:
```python
import math

import jax
import jax.numpy as jnp
from jax import lax
from jax.experimental import pallas as pl
from jax.experimental.pallas import tpu as pltpu
from jax.sharding import PartitionSpec as P

AXES = ("gx", "gy", "gz")
ORDER = ("gx", "gz", "gy")
MESH = pl.DeviceIdType.MESH
F32 = jnp.float32
BF16 = jnp.bfloat16
LANES = 128
DIRECTIONS = [
    (dx, dy, dz)
    for dx in (-1, 0, 1)
    for dy in (-1, 0, 1)
    for dz in (-1, 0, 1)
    if (dx, dy, dz) != (0, 0, 0)
]
CELL_EDGE = 10.0
SOFTENING = 0.3
THOLE_DAMP = 0.39
RELAXATION = 0.7
LN2 = math.log(2.0)
DAMP_ROOT = math.sqrt(THOLE_DAMP / LN2)
RECEIVERS = [(ry, rz) for ry in (0, 1) for rz in (0, 1)]


def away(sizes, axis, step):
    return lax.rem(lax.axis_index(axis) + (step + sizes[axis]), sizes[axis])


def neighbour(sizes, direction):
    return {axis: away(sizes, axis, step) for axis, step in zip(AXES, direction) if step != 0}


def sent_part(step):
    return {0: pl.ds(1, 2), 1: pl.ds(2, 1), -1: pl.ds(1, 1)}[step]


def landing_part(step):
    return {0: pl.ds(1, 2), 1: pl.ds(0, 1), -1: pl.ds(3, 1)}[step]


def halo_copies(sizes, buf, send_sem, recv_sem):
    copies = []
    for number, direction in enumerate(DIRECTIONS):
        dx, dy, dz = direction
        copies.append(
            pltpu.make_async_remote_copy(
                src_ref=buf.at[pl.ds(1, 1), sent_part(dy), sent_part(dz)],
                dst_ref=buf.at[pl.ds(1 - dx, 1), landing_part(dy), landing_part(dz)],
                send_sem=send_sem.at[number],
                recv_sem=recv_sem.at[number],
                device_id=neighbour(sizes, direction),
                device_id_type=MESH,
            )
        )
    return copies


def line_copies(sizes, axis, buf, send_sem, recv_sem):
    me = lax.axis_index(axis)
    copies = []
    for step in range(1, sizes[axis]):
        copies.append(
            pltpu.make_async_remote_copy(
                src_ref=buf.at[me],
                dst_ref=buf.at[me],
                send_sem=send_sem.at[step],
                recv_sem=recv_sem.at[step],
                device_id={axis: away(sizes, axis, step)},
                device_id_type=MESH,
            )
        )
    return copies


def kernel(
    sizes,
    frac_ref,
    pol_ref,
    occ_ref,
    mask_ref,
    perm_ref,
    hist_ref,
    out_ref,
    change_ref,
    geo,
    past,
    masked,
    moved_one,
    moved_two,
    perm_tiles,
    scaled_tiles,
    place,
    ends,
    columns,
    pairs,
    feats,
    *rest,
):
    lines_one, lines_two = rest[0:3], rest[3:6]
    geo_sems, past_sems, dip_sems = rest[6:8], rest[8:10], rest[10:12]
    sems_one = [rest[12 + 2 * n : 14 + 2 * n] for n in range(3)]
    sems_two = [rest[18 + 2 * n : 20 + 2 * n] for n in range(3)]

    barrier = pltpu.get_barrier_semaphore()
    greeted = [neighbour(sizes, direction) for direction in DIRECTIONS]
    for axis in AXES:
        greeted += [{axis: away(sizes, axis, step)} for step in range(2, sizes[axis] - 1)]
    for device in greeted:
        pl.semaphore_signal(barrier, inc=1, device_id=device, device_id_type=MESH)

    lane = lax.broadcasted_iota(jnp.int32, (1, LANES), 1)
    sub = lax.broadcasted_iota(jnp.int32, (8, LANES), 0)

    filled = occ_ref[...].astype(F32)
    filled_rows = jnp.concatenate([filled] * 6, axis=0)
    for h in range(6):
        masked[h] = hist_ref[h] * filled_rows
    for tile, (ry, rz) in enumerate(RECEIVERS):
        own = (1, 1 + ry, 1 + rz)
        weight = jnp.broadcast_to(
            RELAXATION * occ_ref[pl.ds(tile, 1), :].astype(F32) * pol_ref[pl.ds(tile, 1), :],
            (8, LANES),
        )
        scaled_tiles[tile] = jnp.where(lax.rem(sub, 4) == 3, 0.0, weight)
        perm_tiles[tile] = jnp.zeros((8, LANES), F32)
        for which in range(2):
            geo[own + (pl.ds(4 * which, 3),)] = frac_ref[pl.ds(tile, 3, stride=4), :]
            geo[own + (pl.ds(4 * which + 3, 1),)] = pol_ref[pl.ds(tile, 1), :]
            perm_tiles[tile, pl.ds(4 * which, 3), :] = perm_ref[
                pl.ds(12 * which + tile, 3, stride=4), :
            ]
        for h in range(5):
            past[own + (pl.ds(6 * h, 6),)] = masked[h + 1, pl.ds(tile, 6, stride=4), :]
        past[own + (pl.ds(30, 2),)] = jnp.zeros((2, LANES), F32)

    row = jnp.zeros((1, LANES), F32)
    for a in range(6):
        for b in range(a, 6):
            product = masked[a] * masked[b]
            folded = product[0:8] + product[8:16] + product[16:24]
            value = jnp.sum(jnp.sum(folded, axis=0, keepdims=True), axis=1, keepdims=True)
            row = jnp.where(lane == 6 * a + b, value, row)

    def send_line(number, bufs, sems, values):
        axis = ORDER[number]
        bufs[number][lax.axis_index(axis)] = values
        copies = line_copies(sizes, axis, bufs[number], *sems[number])
        for copy in copies:
            copy.start()
        return copies

    def total_line(number, bufs, copies):
        for copy in copies:
            copy.wait_recv()
        return jnp.sum(bufs[number][...], axis=0)

    pl.semaphore_wait(barrier, len(greeted))

    started = []
    line = send_line(0, lines_one, sems_one, row)
    started += line
    geo_copies = halo_copies(sizes, geo, *geo_sems)
    for copy in geo_copies:
        copy.start()
    past_copies = halo_copies(sizes, past, *past_sems)

    row = total_line(0, lines_one, line)
    line = send_line(1, lines_one, sems_one, row)
    started += line
    for copy in past_copies:
        copy.start()
    started += geo_copies + past_copies

    for copy in geo_copies:
        copy.wait_recv()

    slab_row = lax.broadcasted_iota(jnp.int32, (LANES, LANES), 0)
    kind = lax.rem(slab_row, 4)
    tile_y = slab_row // 32
    tile_z = lax.rem(slab_row // 8, 4)
    for sx in range(3):
        shift = jnp.where(
            kind == 0,
            jnp.float32(sx - 1.5),
            jnp.where(kind == 1, (tile_y - 2).astype(F32), (tile_z - 2).astype(F32)),
        )
        slab = geo[sx].reshape(LANES, LANES)
        at = (slab + shift) * CELL_EDGE
        place[sx] = jnp.where(kind == 3, DAMP_ROOT * lax.rsqrt(slab), at)
        ends[sx] = jnp.where(kind == 3, 1.0, at)
        columns[sx] = jnp.transpose(place[sx])

    lane16 = lax.broadcasted_iota(jnp.int32, (16, LANES), 1)
    sub16 = lax.broadcasted_iota(jnp.int32, (16, LANES), 0)

    def pair_block(step, carry):
        sx = step // 8
        block = lax.rem(step, 8)
        first = pl.multiple_of(block * 16, 16)
        cols = columns[sx, pl.ds(first, 16), :]
        apart = jnp.logical_or(sub16 + first != lane16, sx != 1)
        for sy in range(4):
            for sz in range(4):
                at = 8 * (4 * sy + sz)
                source = [
                    jnp.broadcast_to(cols[:, at + n : at + n + 1], (16, LANES)) for n in range(4)
                ]
                for tile, (ry, rz) in enumerate(RECEIVERS):
                    ky, kz = sy - ry, sz - rz
                    if not (0 <= ky <= 2 and 0 <= kz <= 2):
                        continue
                    mine = 8 * (4 * (ry + 1) + rz + 1)
                    d = [source[n] - place[1, pl.ds(mine + n, 1), :] for n in range(3)]
                    damp = source[3] * place[1, pl.ds(mine + 3, 1), :]
                    offset = 9 * sx + 3 * ky + kz
                    allowed = 3.0 * mask_ref[tile, offset].astype(F32)
                    dist = d[0] * d[0] + d[1] * d[1] + d[2] * d[2] + SOFTENING
                    root = lax.rsqrt(dist)
                    inverse = root * root
                    cube = root * inverse * allowed
                    if ky == 1 and kz == 1:
                        cube = jnp.where(apart, cube, 0.0)
                    power = dist * dist * root * damp
                    fade = jnp.exp2(-power)
                    three = 1.0 - fade
                    five = three - (power * LN2) * fade
                    direct = three * cube
                    radial = five * (inverse * cube)
                    base = offset * 256 + first
                    for part, value in ((0, radial), (128, direct)):
                        high = value.astype(BF16)
                        low = (value - high.astype(F32)).astype(BF16)
                        rows = pl.ds(pl.multiple_of(base + part, 16), 16)
                        pairs[tile, rows, pl.ds(0, 128)] = high
                        pairs[tile, rows, pl.ds(128, 128)] = low
        return carry

    lax.fori_loop(0, 12, pair_block, 0)
    row = total_line(1, lines_one, line)
    line = send_line(2, lines_one, sems_one, row)
    started += line
    lax.fori_loop(12, 24, pair_block, 0)
    row = total_line(2, lines_one, line)

    def entry(a, b):
        return jnp.sum(
            jnp.where(lane == 6 * min(a, b) + max(a, b), row, 0.0), axis=1, keepdims=True
        )

    gram = {(a, b): entry(a, b) for a in range(6) for b in range(a, 6) if a < 5}
    trace = gram[0, 0] + gram[1, 1] + gram[2, 2] + gram[3, 3] + gram[4, 4]
    ridge = 0.001 * trace / 5.0 + 1.0
    low = {}
    scale = []
    half = []
    for a in range(5):
        pivot = gram[a, a] + ridge
        for c in range(a):
            pivot = pivot - low[a, c] * low[a, c]
        scale.append(lax.rsqrt(pivot))
        for b in range(a + 1, 5):
            value = gram[a, b]
            for c in range(a):
                value = value - low[a, c] * low[b, c]
            low[b, a] = value * scale[a]
        value = gram[a, 5]
        for c in range(a):
            value = value - low[a, c] * half[c]
        half.append(value * scale[a])
    coeffs = [None] * 5
    for a in reversed(range(5)):
        value = half[a]
        for b in range(a + 1, 5):
            value = value - low[b, a] * coeffs[b]
        coeffs[a] = value * scale[a]
    coeffs = [jnp.broadcast_to(value, (8, LANES))[0:6] for value in coeffs]

    for copy in past_copies:
        copy.wait_recv()

    first_set = sub < 4

    def write_feats(sx, s, tile_ref):
        whole = tile_ref[...]
        near = ends[sx, pl.ds(pl.multiple_of(8 * s, 8), 8), :]
        multipliers = []
        along = None
        for b in range(3):
            both = jnp.where(first_set, whole[b : b + 1], whole[4 + b : 5 + b])
            multipliers.append(both)
            term = near[b : b + 1] * both
            along = term if along is None else along + term
        multipliers.append(along)
        parts = [near * value for value in multipliers]
        flat = jnp.zeros((8, LANES), F32)
        for half_at in range(2):
            value = jnp.concatenate(parts[2 * half_at : 2 * half_at + 2], axis=0)
            other = jnp.concatenate(
                [flat, whole * (-1.0 / 3.0) if half_at == 1 else flat], axis=0
            )
            for piece in range(3):
                rows = pl.ds(32 * piece + 16 * half_at, 16)
                kept = value.astype(BF16)
                feats[sx, s, rows, pl.ds(0, 128)] = kept
                value = value - kept.astype(F32)
                kept = other.astype(BF16)
                feats[sx, s, rows, pl.ds(128, 128)] = kept
                other = other - kept.astype(F32)

    def predict(number, carry):
        sx, s = number // 16, lax.rem(number, 16)
        sy, sz = s // 4, lax.rem(s, 4)
        total = None
        for h in range(5):
            term = coeffs[h] * past[sx, sy, sz, pl.ds(6 * h, 6), :]
            total = term if total is None else total + term
        moved_one[sx, sy, sz] = jnp.zeros((8, LANES), F32)
        moved_one[sx, sy, sz, pl.ds(0, 3), :] = total[0:3]
        moved_one[sx, sy, sz, pl.ds(4, 3), :] = total[3:6]
        write_feats(sx, s, moved_one.at[sx, sy, sz])
        return carry

    lax.fori_loop(0, 48, predict, 0)

    def field(tile):
        ry, rz = RECEIVERS[tile]
        summed = None
        for kx in range(3):
            lhs = jnp.concatenate(
                [feats[kx, 4 * (ry + ky) + rz + kz] for ky in range(3) for kz in range(3)], axis=1
            )
            part = jnp.dot(
                lhs, pairs[tile, pl.ds(2304 * kx, 2304), :], preferred_element_type=F32
            )
            summed = part if summed is None else summed + part
        both = summed[:, 0:128] + summed[:, 128:256]
        out = both[0:32] + both[32:64] + both[64:96]
        mine = 8 * (4 * (ry + 1) + rz + 1)
        here = ends[1, pl.ds(mine, 8), :]
        value = out[24:32]
        for b in range(3):
            value = value - here[b : b + 1] * out[8 * b : 8 * b + 8]
        shared = jnp.where(first_set, value[3:4], value[7:8])
        return value - here * shared

    def relaxed(tile, before):
        return (1.0 - RELAXATION) * before + scaled_tiles[tile] * (perm_tiles[tile] + field(tile))

    for tile, (ry, rz) in enumerate(RECEIVERS):
        moved_two[1, 1 + ry, 1 + rz] = relaxed(tile, moved_one[1, 1 + ry, 1 + rz])

    dip_copies = halo_copies(sizes, moved_two, *dip_sems)
    for copy in dip_copies:
        copy.start()
    started += dip_copies
    for copy in dip_copies:
        copy.wait_recv()

    def second(number, carry):
        sx, s = number // 16, lax.rem(number, 16)
        write_feats(sx, s, moved_two.at[sx, s // 4, lax.rem(s, 4)])
        return carry

    lax.fori_loop(0, 48, second, 0)

    changed = jnp.zeros((8, LANES), F32)
    size = jnp.zeros((8, LANES), F32)
    for tile, (ry, rz) in enumerate(RECEIVERS):
        before = moved_two[1, 1 + ry, 1 + rz]
        after = relaxed(tile, before)
        out_ref[pl.ds(tile, 3, stride=4), :] = after[0:3]
        out_ref[pl.ds(12 + tile, 3, stride=4), :] = after[4:7]
        update = after - before
        changed = changed + update * update
        size = size + after * after

    def whole_sum(value):
        return jnp.sum(jnp.sum(value, axis=0, keepdims=True), axis=1, keepdims=True)

    row = jnp.where(lane == 0, whole_sum(changed), jnp.where(lane == 1, whole_sum(size), 0.0))
    for number in range(3):
        line = send_line(number, lines_two, sems_two, row)
        started += line
        row = total_line(number, lines_two, line)
    top = jnp.sum(jnp.where(lane == 0, row, 0.0), axis=1, keepdims=True)
    bottom = jnp.sum(jnp.where(lane == 1, row, 0.0), axis=1, keepdims=True)
    change_ref[...] = jnp.broadcast_to(jnp.sqrt(top / (bottom + 1.0)), (1, LANES))

    for copy in started:
        copy.wait_send()


def on_device(sizes, fractions, polarizability, occupancy, pair_mask, perm_field, history):
    vmem = pl.BlockSpec(memory_space=pltpu.VMEM)
    smem = pl.BlockSpec(memory_space=pltpu.SMEM)
    dma = pltpu.SemaphoreType.DMA
    line_bufs = [pltpu.VMEM((sizes[axis], 1, LANES), F32) for axis in ORDER]
    line_sems = []
    for axis in ORDER:
        line_sems += [dma((sizes[axis],)), dma((sizes[axis],))]
    scratch = [
        pltpu.VMEM((3, 4, 4, 8, LANES), F32),
        pltpu.VMEM((3, 4, 4, 32, LANES), F32),
        pltpu.VMEM((6, 24, LANES), F32),
        pltpu.VMEM((3, 4, 4, 8, LANES), F32),
        pltpu.VMEM((3, 4, 4, 8, LANES), F32),
        pltpu.VMEM((4, 8, LANES), F32),
        pltpu.VMEM((4, 8, LANES), F32),
        pltpu.VMEM((3, LANES, LANES), F32),
        pltpu.VMEM((3, LANES, LANES), F32),
        pltpu.VMEM((3, LANES, LANES), F32),
        pltpu.VMEM((4, 27 * 256, 256), BF16),
        pltpu.VMEM((3, 16, 96, 256), BF16),
    ]
    scratch += line_bufs + line_bufs + [dma((26,))] * 6 + line_sems + line_sems
    induced, change = pl.pallas_call(
        lambda *refs: kernel(sizes, *refs),
        out_shape=(
            jax.ShapeDtypeStruct((24, LANES), F32),
            jax.ShapeDtypeStruct((1, LANES), F32),
        ),
        in_specs=[vmem, vmem, vmem, smem, vmem, vmem],
        out_specs=(vmem, vmem),
        scratch_shapes=scratch,
        compiler_params=pltpu.CompilerParams(
            collective_id=0, has_side_effects=True, vmem_limit_bytes=60 * 1024 * 1024
        ),
    )(
        fractions.reshape(12, LANES),
        polarizability.reshape(4, LANES),
        occupancy.reshape(4, LANES),
        pair_mask.reshape(4, 27),
        perm_field.reshape(24, LANES),
        history.reshape(6, 24, LANES),
    )
    return induced.reshape(6, 1, 2, 2, LANES), change[0, 0]


def solution(mesh):
    sizes = {axis: mesh.shape[axis] for axis in AXES}
    placed = (
        P(None, "gx", "gy", "gz", None),
        P("gx", "gy", "gz", None),
        P("gx", "gy", "gz", None),
        P("gx", "gy", "gz", None),
        P(None, "gx", "gy", "gz", None),
        P(None, None, "gx", "gy", "gz", None),
    )
    return jax.shard_map(
        lambda *args: on_device(sizes, *args),
        mesh=mesh,
        in_specs=placed,
        out_specs=(P(None, "gx", "gy", "gz", None), P()),
        check_vma=False,
    )
```

time: 433 us -> 64 us (0.15); the launches traced: 427 us -> 63.4 us
  other arithmetic: 223 us -> 0 us
  blocking collectives: 89.3 us -> 0 us
  Pallas kernels: 0 us -> 59 us
  local copies, waits for them, and re-layouts: 45.7 us -> 2.6 us
  starting transfers between devices: 43.1 us -> 0 us
  loops' own time: 10.2 us -> 0 us
  waiting for transfers between devices: 9.63 us -> 0 us
    slice x54 -> x0, other arithmetic: 104 us -> none  [pair_field(): moment[3 * which_set + axis_num][:, None, :]]
    reduce_sum x110 -> x0, other arithmetic: 104 us -> none  [the longest x108 102 us: pair_field(): jnp.sum(radial * project * displace[axis_num] - direct * parts[axis_num],...]
    psum x8 -> x0, blocking collectives: 89.3 us -> none  [one_axis_at_a_time(): return functools.reduce(lax.psum, axes, shard)]
    pallas_call x0 -> x1, Pallas kernels: none -> 59 us  [on_device(): pl.pallas_call(lambda *refs: kernel(sizes, *refs), out_shape=(jax.ShapeDt...]
    ppermute x12 -> x0, starting transfers between devices: 43.1 us -> none  [the longest x6 23.9 us: with_halo(): lax.ppermute(head, axis, [((i + 1) % count, i) for i in range(count)])]
    slice x62 -> x0, local copies, waits for them, and re-layouts: 36.5 us -> none  [the longest x54 36 us: pair_field(): offset_vec[axis_num] + source[axis_num][:, None, :]]
    another operation x2 -> x0, loops' own time: 10.2 us -> none  [slab_field(): lax.fori_loop(0, 27, offset_step, jnp.zeros((rows, width_y * width_z, slo...]
    ppermute x12 -> x0, waiting for transfers between devices: 9.63 us -> none  [the longest x6 7.49 us: with_halo(): lax.ppermute(head, axis, [((i + 1) % count, i) for i in range(count)])]
  transfers between devices with their start and end apart: 12 -> 0, of which waited for: 8 -> 0; matrix products, arithmetic and copies ran while one was open for 1% -> 0% of each run, Pallas kernels for 0% -> 0%
where the time goes in v1:
time: 64 us; the launch traced here: 63.4 us
  Pallas kernels  59 us (92%)
  local copies, waits for them, and re-layouts  2.6 us (4%)
  between operations  1.82 us (3%)
    pallas_call x1, Pallas kernels, on_device(): pl.pallas_call(lambda *refs: kernel(sizes, *refs), out_shape=(jax.ShapeDt...  59 us
    unnamed x5, local copies, waits for them, and re-layouts  2 us

profile of v1, /device:TPU:1, one launch (start us, length us, event | category | flops | bytes accessed | tf_op | source)
XLA Modules:
  0.0 63.4 jit_solution(6127852848283163199)
XLA Ops:
  0.6 0.0 copy-start
  0.6 0.7 %copy-done = f32[3,1,2,2,128]{4,3,2,1,0:T(2,128)S(1)} copy-done((f32[3,1,2,2,128]{4,3,2,1,0:T(2,128)S(1)}, f32[3,1,2,2,128]{4,3,2,1,0:T(2,128)}, u32[]{:S(2)}) %copy-start) | copy-done | bytes 6168
  1.3 0.6 reshape.25.refs_0_
  1.9 59.0 %shard_map.77 = (f32[24,128]{1,0:T(8,128)}, f32[1,128]{1,0:T(1,128)}) custom-call(f32[12,128]{1,0:T(8,128)} %reshape.25.refs_0_, f32[4,128]{1,0:T(4,128)} %bitcast.13, s32[4,128]{1,0:T(4,128)} %bitcast.14, s32[4,27]{1,0:T(4,128)} %bitcast.15, f32[24,128]{1,0:T(8,128)} %bitcast.11, f32[6,24,128]{2,1,0:T(8,128)} %bitcast.10), custom_call_target="tpu_custom_call" | custom-call | tf_op jit(solution)/shard_map/pallas_call | solution.py:423
  60.9 0.0 copy-start.1
  61.0 1.3 %copy.11 = f32[6,1,2,2,128]{4,3,2,1,0:T(2,128)} copy(f32[6,1,2,2,128]{4,3,2,1,0:T(2,128)} %bitcast.12) | data formatting | bytes 24576
  62.3 0.0 copy-done.1
Async XLA Ops:
  0.6 0.7 %copy-start = (f32[3,1,2,2,128]{4,3,2,1,0:T(2,128)S(1)}, f32[3,1,2,2,128]{4,3,2,1,0:T(2,128)}, u32[]{:S(2)}) copy-start(f32[3,1,2,2,128]{4,3,2,1,0:T(2,128)} %param.6) | copy-start | bytes 18436
  60.9 1.3 %copy-start.1 = (f32[1,128]{1,0:T(1,128)S(1)}, f32[1,128]{1,0:T(1,128)}, u32[]{:S(2)}) copy-start(f32[1,128]{1,0:T(1,128)} %get-tuple-element.5) | copy-start | bytes 1540

commit v2 on v1

v2 whole, which is shorter than its diff:
```python
import math

import jax
import jax.numpy as jnp
from jax import lax
from jax.experimental import pallas as pl
from jax.experimental.pallas import tpu as pltpu
from jax.sharding import PartitionSpec as P

AXES = ("gx", "gy", "gz")
FIRST_GROUPS = (("gx",), ("gz",), ("gy",))
LAST_GROUPS = (("gx",), ("gy", "gz"))
MESH = pl.DeviceIdType.MESH
F32 = jnp.float32
BF16 = jnp.bfloat16
LANES = 128
DIRECTIONS = [
    (dx, dy, dz)
    for dx in (-1, 0, 1)
    for dy in (-1, 0, 1)
    for dz in (-1, 0, 1)
    if (dx, dy, dz) != (0, 0, 0)
]
CELL_EDGE = 10.0
SOFTENING = 0.3
THOLE_DAMP = 0.39
RELAXATION = 0.7
LN2 = math.log(2.0)
DAMP_ROOT = math.sqrt(THOLE_DAMP / LN2)
RECEIVERS = [(ry, rz) for ry in (0, 1) for rz in (0, 1)]


SEMS = 8 + len(FIRST_GROUPS) + len(LAST_GROUPS)
VMEM_BYTES = 62 * 1000 * 1000


def away(sizes, axis, step):
    return lax.rem(lax.axis_index(axis) + (step + sizes[axis]), sizes[axis])


def neighbour(sizes, direction):
    return {axis: away(sizes, axis, step) for axis, step in zip(AXES, direction) if step != 0}


def sent_part(step):
    return {0: pl.ds(1, 2), 1: pl.ds(2, 1), -1: pl.ds(1, 1)}[step]


def landing_part(step):
    return {0: pl.ds(1, 2), 1: pl.ds(0, 1), -1: pl.ds(3, 1)}[step]


def remote(src, dst, sems, device):
    return pltpu.make_async_remote_copy(
        src_ref=src,
        dst_ref=dst,
        send_sem=sems[0],
        recv_sem=sems[1],
        device_id=device,
        device_id_type=MESH,
    )


class Batch:
    def __init__(self, copies, counted, sems, device):
        self.copies = copies
        self.whole = remote(counted, counted, sems, device)

    def start(self):
        for copy in self.copies:
            copy.start()

    def arrived(self):
        self.whole.wait_recv()

    def sent(self):
        self.whole.wait_send()


def halo_batch(sizes, buf, sems, same_slab):
    copies = []
    for direction in DIRECTIONS:
        dx, dy, dz = direction
        if (dx == 0) != same_slab:
            continue
        copies.append(
            remote(
                buf.at[pl.ds(1, 1), sent_part(dy), sent_part(dz)],
                buf.at[pl.ds(1 - dx, 1), landing_part(dy), landing_part(dz)],
                sems,
                neighbour(sizes, direction),
            )
        )
    counted = buf.at[1, pl.ds(0, 3)] if same_slab else buf.at[pl.ds(0, 2)]
    return Batch(copies, counted, sems, neighbour(sizes, (0, 0, 1)))


def tile_batch(sizes, buf, sems, tile, counted):
    ry, rz = RECEIVERS[tile]
    mine = buf.at[1, 1 + ry, 1 + rz]
    copies = []
    for dx in (-1, 0, 1):
        for dy, at_y in ((0, 1 + ry), (2 * ry - 1, 3 - 3 * ry)):
            for dz, at_z in ((0, 1 + rz), (2 * rz - 1, 3 - 3 * rz)):
                if (dx, dy, dz) != (0, 0, 0):
                    copies.append(
                        remote(
                            mine,
                            buf.at[1 - dx, at_y, at_z],
                            sems,
                            neighbour(sizes, (dx, dy, dz)),
                        )
                    )
    return Batch(copies, counted, sems, neighbour(sizes, (0, 0, 1)))


def group_steps(sizes, axes):
    steps = [()]
    for axis in axes:
        steps = [step + (n,) for step in steps for n in range(sizes[axis])]
    far = lambda step: sum(min(n, sizes[axis] - n) for n, axis in zip(step, axes))
    return sorted([step for step in steps if any(step)], key=far, reverse=True)


def group_batch(sizes, axes, buf, sems):
    me = 0
    for axis in axes:
        me = me * sizes[axis] + lax.axis_index(axis)
    copies = []
    for step in group_steps(sizes, axes):
        device = {axis: away(sizes, axis, n) for axis, n in zip(axes, step) if n != 0}
        copies.append(remote(buf.at[me], buf.at[me], sems, device))
    counted = buf.at[pl.ds(0, len(copies))]
    return me, Batch(copies, counted, sems, {axes[0]: away(sizes, axes[0], 1)})


def kernel(
    sizes,
    frac_hbm,
    pol_hbm,
    occ_hbm,
    mask_hbm,
    perm_hbm,
    hist_hbm,
    out_ref,
    change_ref,
    frac_ref,
    pol_ref,
    occ_ref,
    mask_ref,
    perm_ref,
    hist_ref,
    own_geo,
    geo,
    past,
    masked,
    moved_one,
    moved_two,
    perm_tiles,
    scaled_tiles,
    receiver,
    ends,
    own_columns,
    columns,
    pairs,
    feats,
    partial,
    counted,
    in_sems,
    send_sems,
    recv_sems,
    *lines,
):
    lines_one, lines_two = lines[: len(FIRST_GROUPS)], lines[len(FIRST_GROUPS) :]
    sems = [(send_sems.at[n], recv_sems.at[n]) for n in range(SEMS)]

    loads = [
        pltpu.make_async_copy(src, dst, in_sems.at[n])
        for n, (src, dst) in enumerate(
            (
                (frac_hbm, frac_ref),
                (pol_hbm, pol_ref),
                (occ_hbm, occ_ref),
                (hist_hbm, hist_ref),
                (mask_hbm, mask_ref),
                (perm_hbm, perm_ref),
            )
        )
    ]
    for load in loads:
        load.start()

    barrier = pltpu.get_barrier_semaphore()
    greeted = [neighbour(sizes, direction) for direction in DIRECTIONS]
    for axis in AXES:
        greeted += [{axis: away(sizes, axis, step)} for step in range(2, sizes[axis] - 1)]
    for device in greeted:
        pl.semaphore_signal(barrier, inc=1, device_id=device, device_id_type=MESH)

    lane = lax.broadcasted_iota(jnp.int32, (1, LANES), 1)
    sub = lax.broadcasted_iota(jnp.int32, (8, LANES), 0)
    lane16 = lax.broadcasted_iota(jnp.int32, (16, LANES), 1)
    sub16 = lax.broadcasted_iota(jnp.int32, (16, LANES), 0)

    loads[0].wait()
    loads[1].wait()
    for tile, (ry, rz) in enumerate(RECEIVERS):
        for which in range(2):
            for c in range(3):
                own_geo[tile, pl.ds(4 * which + c, 1)] = frac_ref[c, pl.ds(tile, 1), :]
            own_geo[tile, pl.ds(4 * which + 3, 1)] = pol_ref[pl.ds(tile, 1), :]
        geo[1, 1 + ry, 1 + rz] = own_geo[tile]

    def positions(slab, rows, sx, tile_y, tile_z):
        kind = lax.rem(rows, 4)
        shift = jnp.where(
            kind == 0,
            jnp.float32(sx - 1.5),
            jnp.where(kind == 1, (tile_y - 2).astype(F32), (tile_z - 2).astype(F32)),
        )
        at = (slab + shift) * CELL_EDGE
        return kind == 3, at, DAMP_ROOT * lax.rsqrt(slab)

    row32 = lax.broadcasted_iota(jnp.int32, (32, LANES), 0)
    last, at, root = positions(
        own_geo[...].reshape(32, LANES), row32, 1, 1 + row32 // 16, 1 + lax.rem(row32 // 8, 2)
    )
    receiver[...] = jnp.where(last, -root, at)
    own_columns[...] = jnp.transpose(
        jnp.concatenate([jnp.where(last, root, at), jnp.zeros((96, LANES), F32)], axis=0)
    )

    def pair_factors(cols, places, offset_of, sx, first):
        for at, sy, sz in places:
            source = [
                jnp.broadcast_to(cols[:, at + n : at + n + 1], (16, LANES)) for n in range(4)
            ]
            for tile, (ry, rz) in enumerate(RECEIVERS):
                ky, kz = sy - ry, sz - rz
                if not (0 <= ky <= 2 and 0 <= kz <= 2):
                    continue
                d = [source[n] - receiver[pl.ds(8 * tile + n, 1), :] for n in range(3)]
                damp = source[3] * receiver[pl.ds(8 * tile + 3, 1), :]
                offset = 9 * sx + 3 * ky + kz
                allowed = 3.0 * mask_ref[tile, offset].astype(F32)
                dist = d[0] * d[0] + d[1] * d[1] + d[2] * d[2] + SOFTENING
                root = lax.rsqrt(dist)
                inverse = root * root
                cube = root * inverse * allowed
                if offset_of == "own" and ky == 1 and kz == 1:
                    cube = jnp.where(sub16 + first != lane16, cube, 0.0)
                power = dist * dist * root * damp
                fade = jnp.exp2(power)
                three = 1.0 - fade
                five = three + (power * LN2) * fade
                for part, value in ((0, five * (inverse * cube)), (128, three * cube)):
                    high = value.astype(BF16)
                    low = (value - high.astype(F32)).astype(BF16)
                    rows = pl.ds(pl.multiple_of(first + part, 16), 16)
                    pairs[tile, offset, rows, pl.ds(0, 128)] = high
                    pairs[tile, offset, rows, pl.ds(128, 128)] = low

    loads[2].wait()
    loads[3].wait()
    filled = occ_ref[...].astype(F32)
    filled_rows = jnp.concatenate([filled] * 6, axis=0)
    for h in range(6):
        masked[h] = hist_ref[h] * filled_rows
    row = jnp.zeros((1, LANES), F32)
    for a in range(6):
        for b in range(a, 6):
            product = masked[a] * masked[b]
            folded = product[0:8] + product[8:16] + product[16:24]
            value = jnp.sum(jnp.sum(folded, axis=0, keepdims=True), axis=1, keepdims=True)
            row = jnp.where(lane == 6 * a + b, value, row)

    for tile, (ry, rz) in enumerate(RECEIVERS):
        own = (1, 1 + ry, 1 + rz)
        for h in range(5):
            past[own + (pl.ds(6 * h, 6),)] = masked[h + 1, pl.ds(tile, 6, stride=4), :]
        past[own + (pl.ds(30, 2),)] = jnp.zeros((2, LANES), F32)

    loads[4].wait()
    loads[5].wait()
    for tile in range(4):
        weight = jnp.broadcast_to(
            RELAXATION * occ_ref[pl.ds(tile, 1), :].astype(F32) * pol_ref[pl.ds(tile, 1), :],
            (8, LANES),
        )
        scaled_tiles[tile] = jnp.where(lax.rem(sub, 4) == 3, 0.0, weight)
        perm_tiles[tile] = jnp.zeros((8, LANES), F32)
        for which in range(2):
            perm_tiles[tile, pl.ds(4 * which, 3), :] = perm_ref[
                pl.ds(12 * which + tile, 3, stride=4), :
            ]

    own_places = [(8 * tile, 1 + ry, 1 + rz) for tile, (ry, rz) in enumerate(RECEIVERS)]
    all_places = [(8 * (4 * sy + sz), sy, sz) for sy in range(4) for sz in range(4)]
    rim_places = [(at, sy, sz) for at, sy, sz in all_places if sy in (0, 3) or sz in (0, 3)]

    def own_block(block, carry):
        first = pl.multiple_of(block * 16, 16)
        pair_factors(own_columns[pl.ds(first, 16), :], own_places, "own", 1, first)
        return carry

    lax.fori_loop(0, 8, own_block, 0)

    def clear(number, carry):
        sx, s = number // 16, lax.rem(number, 16)
        for piece in range(3):
            feats[sx, s, pl.ds(32 * piece, 16), pl.ds(128, 128)] = jnp.zeros((16, LANES), BF16)
        return carry

    lax.fori_loop(0, 48, clear, 0, unroll=4)

    def send_group(groups, number, bufs, first_sem, values):
        me, batch = group_batch(sizes, groups[number], bufs[number], sems[first_sem + number])
        bufs[number][me] = values
        batch.start()
        return batch

    def total(bufs, number, batch):
        batch.arrived()
        return jnp.sum(bufs[number][...], axis=0)

    pl.semaphore_wait(barrier, len(greeted))

    geo_batches = [halo_batch(sizes, geo, sems[n], n == 0) for n in range(2)]
    past_batches = [halo_batch(sizes, past, sems[2 + n], n == 0) for n in range(2)]
    line_a = send_group(FIRST_GROUPS, 0, lines_one, 8, row)
    for batch in geo_batches + past_batches:
        batch.start()

    row128 = lax.broadcasted_iota(jnp.int32, (LANES, LANES), 0)

    def place_slab(sx):
        last, at, root = positions(
            geo[sx].reshape(LANES, LANES), row128, sx, row128 // 32, lax.rem(row128 // 8, 4)
        )
        ends[sx] = jnp.where(last, 1.0, at)
        columns[sx] = jnp.transpose(jnp.where(last, root, at))

    geo_batches[0].arrived()
    place_slab(1)

    def rim_block(block, carry):
        first = pl.multiple_of(block * 16, 16)
        pair_factors(columns[1, pl.ds(first, 16), :], rim_places, "rim", 1, first)
        return carry

    lax.fori_loop(0, 8, rim_block, 0)

    row = total(lines_one, 0, line_a)
    line_b = send_group(FIRST_GROUPS, 1, lines_one, 8, row)

    geo_batches[1].arrived()
    place_slab(0)
    place_slab(2)

    def side_block(step, carry):
        sx = 2 * (step // 8)
        first = pl.multiple_of(lax.rem(step, 8) * 16, 16)
        pair_factors(columns[sx, pl.ds(first, 16), :], all_places, "side", sx, first)
        return carry

    lax.fori_loop(0, 11, side_block, 0)
    row = total(lines_one, 1, line_b)
    line_c = send_group(FIRST_GROUPS, 2, lines_one, 8, row)
    lax.fori_loop(11, 16, side_block, 0)
    row = total(lines_one, 2, line_c)

    def entry(a, b):
        return jnp.sum(
            jnp.where(lane == 6 * min(a, b) + max(a, b), row, 0.0), axis=1, keepdims=True
        )

    gram = {(a, b): entry(a, b) for a in range(6) for b in range(a, 6) if a < 5}
    trace = gram[0, 0] + gram[1, 1] + gram[2, 2] + gram[3, 3] + gram[4, 4]
    ridge = 0.001 * trace / 5.0 + 1.0
    low = {}
    scale = []
    half = []
    for a in range(5):
        pivot = gram[a, a] + ridge
        for c in range(a):
            pivot = pivot - low[a, c] * low[a, c]
        scale.append(lax.rsqrt(pivot))
        for b in range(a + 1, 5):
            value = gram[a, b]
            for c in range(a):
                value = value - low[a, c] * low[b, c]
            low[b, a] = value * scale[a]
        value = gram[a, 5]
        for c in range(a):
            value = value - low[a, c] * half[c]
        half.append(value * scale[a])
    coeffs = [None] * 5
    for a in reversed(range(5)):
        value = half[a]
        for b in range(a + 1, 5):
            value = value - low[b, a] * coeffs[b]
        coeffs[a] = value * scale[a]
    coeffs = [jnp.broadcast_to(value, (8, LANES))[0:6] for value in coeffs]

    past_batches[0].arrived()
    past_batches[1].arrived()

    first_set = sub < 4
    flat = jnp.zeros((8, LANES), F32)

    def write_feats(sx, s, tile_ref):
        whole = tile_ref[...]
        near = ends[sx, pl.ds(8 * s, 8), :]
        multipliers = []
        along = None
        for b in range(3):
            both = jnp.where(first_set, whole[b : b + 1], whole[4 + b : 5 + b])
            multipliers.append(both)
            term = near[b : b + 1] * both
            along = term if along is None else along + term
        multipliers.append(along)
        parts = [near * value for value in multipliers]
        for half_at in range(2):
            value = jnp.concatenate(parts[2 * half_at : 2 * half_at + 2], axis=0)
            for piece in range(3):
                kept = value.astype(BF16)
                feats[sx, s, pl.ds(32 * piece + 16 * half_at, 16), pl.ds(0, 128)] = kept
                value = value - kept.astype(F32)
        value = jnp.concatenate([flat, whole * (-1.0 / 3.0)], axis=0)
        for piece in range(3):
            kept = value.astype(BF16)
            feats[sx, s, pl.ds(32 * piece + 16, 16), pl.ds(128, 128)] = kept
            value = value - kept.astype(F32)

    def predict(sx, carry):
        for s in range(16):
            sy, sz = s // 4, s % 4
            value = None
            for h in range(5):
                term = coeffs[h] * past[sx, sy, sz, pl.ds(6 * h, 6), :]
                value = term if value is None else value + term
            moved_one[sx, sy, sz] = flat
            moved_one[sx, sy, sz, pl.ds(0, 3), :] = value[0:3]
            moved_one[sx, sy, sz, pl.ds(4, 3), :] = value[3:6]
        for s in range(16):
            write_feats(sx, s, moved_one.at[sx, s // 4, s % 4])
        return carry

    lax.fori_loop(0, 3, predict, 0)

    def dot_part(tile, sources):
        ry, rz = RECEIVERS[tile]
        lhs = jnp.concatenate([feats[sx, 4 * sy + sz] for sx, sy, sz in sources], axis=1)
        rhs = jnp.concatenate(
            [pairs[tile, 9 * sx + 3 * (sy - ry) + sz - rz] for sx, sy, sz in sources], axis=0
        )
        return jnp.dot(lhs, rhs, preferred_element_type=F32)

    def sources_of(tile, kinds=None):
        ry, rz = RECEIVERS[tile]
        return [
            (sx, ry + ky, rz + kz)
            for sx in range(3)
            for ky in range(3)
            for kz in range(3)
            if kinds is None or ((ry + ky + 1) % 2, (rz + kz + 1) % 2) == kinds
        ]

    def relaxed(tile, before, summed):
        both = summed[:, 0:128] + summed[:, 128:256]
        out = both[0:32] + both[32:64] + both[64:96]
        ry, rz = RECEIVERS[tile]
        here = ends[1, pl.ds(8 * (4 * (ry + 1) + rz + 1), 8), :]
        value = out[24:32]
        for b in range(3):
            value = value - here[b : b + 1] * out[8 * b : 8 * b + 8]
        shared = jnp.where(first_set, value[3:4], value[7:8])
        field = value - here * shared
        return (1.0 - RELAXATION) * before + scaled_tiles[tile] * (perm_tiles[tile] + field)

    tile_batches = []
    for tile, (ry, rz) in enumerate(RECEIVERS):
        before = moved_one[1, 1 + ry, 1 + rz]
        moved_two[1, 1 + ry, 1 + rz] = relaxed(tile, before, dot_part(tile, sources_of(tile)))
        tile_batches.append(tile_batch(sizes, moved_two, sems[4 + tile], tile, counted))
        tile_batches[-1].start()

    for batch in geo_batches + past_batches + [line_a, line_b, line_c]:
        batch.sent()

    changed = flat
    size = flat
    for kind, kinds in enumerate(RECEIVERS):
        tile_batches[kind].arrived()
        tiles = [
            (sy, sz)
            for sy in range(4)
            for sz in range(4)
            if ((sy + 1) % 2, (sz + 1) % 2) == kinds
        ]
        for sx in range(3):
            for sy, sz in tiles:
                write_feats(sx, 4 * sy + sz, moved_two.at[sx, sy, sz])
        for tile, (ry, rz) in enumerate(RECEIVERS):
            summed = dot_part(tile, sources_of(tile, kinds))
            if kind > 0:
                summed = summed + partial[tile]
            if kind < 3:
                partial[tile] = summed
                continue
            before = moved_two[1, 1 + ry, 1 + rz]
            after = relaxed(tile, before, summed)
            out_ref[pl.ds(tile, 3, stride=4), :] = after[0:3]
            out_ref[pl.ds(12 + tile, 3, stride=4), :] = after[4:7]
            update = after - before
            changed = changed + update * update
            size = size + after * after

    def whole_sum(value):
        return jnp.sum(jnp.sum(value, axis=0, keepdims=True), axis=1, keepdims=True)

    row = jnp.where(lane == 0, whole_sum(changed), jnp.where(lane == 1, whole_sum(size), 0.0))
    ending = []
    for number in range(len(LAST_GROUPS)):
        ending.append(send_group(LAST_GROUPS, number, lines_two, 8 + len(FIRST_GROUPS), row))
        if number == 0:
            for batch in tile_batches:
                batch.sent()
        row = total(lines_two, number, ending[-1])
    top = jnp.sum(jnp.where(lane == 0, row, 0.0), axis=1, keepdims=True)
    bottom = jnp.sum(jnp.where(lane == 1, row, 0.0), axis=1, keepdims=True)
    change_ref[...] = jnp.broadcast_to(jnp.sqrt(top / (bottom + 1.0)), (1, LANES))

    for batch in ending:
        batch.sent()


def on_device(sizes, fractions, polarizability, occupancy, pair_mask, perm_field, history):
    vmem = pl.BlockSpec(memory_space=pltpu.VMEM)
    hbm = pl.BlockSpec(memory_space=pltpu.HBM)
    dma = pltpu.SemaphoreType.DMA
    line_bufs = [
        pltpu.VMEM((math.prod(sizes[axis] for axis in axes), 1, LANES), F32)
        for axes in FIRST_GROUPS + LAST_GROUPS
    ]
    scratch = [
        pltpu.VMEM((3, 4, LANES), F32),
        pltpu.VMEM((4, LANES), F32),
        pltpu.VMEM((4, LANES), jnp.int32),
        pltpu.SMEM((4, 27), jnp.int32),
        pltpu.VMEM((24, LANES), F32),
        pltpu.VMEM((6, 24, LANES), F32),
        pltpu.VMEM((4, 8, LANES), F32),
        pltpu.VMEM((3, 4, 4, 8, LANES), F32),
        pltpu.VMEM((3, 4, 4, 32, LANES), F32),
        pltpu.VMEM((6, 24, LANES), F32),
        pltpu.VMEM((3, 4, 4, 8, LANES), F32),
        pltpu.VMEM((3, 4, 4, 8, LANES), F32),
        pltpu.VMEM((4, 8, LANES), F32),
        pltpu.VMEM((4, 8, LANES), F32),
        pltpu.VMEM((32, LANES), F32),
        pltpu.VMEM((3, LANES, LANES), F32),
        pltpu.VMEM((LANES, LANES), F32),
        pltpu.VMEM((3, LANES, LANES), F32),
        pltpu.VMEM((4, 27, 256, 256), BF16),
        pltpu.VMEM((3, 16, 96, 256), BF16),
        pltpu.VMEM((4, 96, 256), F32),
        pltpu.VMEM((11, 8, LANES), F32),
        dma((6,)),
        dma((SEMS,)),
        dma((SEMS,)),
    ]
    induced, change = pl.pallas_call(
        lambda *refs: kernel(sizes, *refs),
        out_shape=(
            jax.ShapeDtypeStruct((24, LANES), F32),
            jax.ShapeDtypeStruct((1, LANES), F32),
        ),
        in_specs=[hbm] * 6,
        out_specs=(vmem, vmem),
        scratch_shapes=scratch + line_bufs,
        compiler_params=pltpu.CompilerParams(
            collective_id=0, has_side_effects=True, vmem_limit_bytes=VMEM_BYTES
        ),
    )(
        fractions.reshape(3, 4, LANES),
        polarizability.reshape(4, LANES),
        occupancy.reshape(4, LANES),
        pair_mask.reshape(4, 27),
        perm_field.reshape(24, LANES),
        history.reshape(6, 24, LANES),
    )
    return induced.reshape(6, 1, 2, 2, LANES), change[0, 0]


def solution(mesh):
    sizes = {axis: mesh.shape[axis] for axis in AXES}
    placed = (
        P(None, "gx", "gy", "gz", None),
        P("gx", "gy", "gz", None),
        P("gx", "gy", "gz", None),
        P("gx", "gy", "gz", None),
        P(None, "gx", "gy", "gz", None),
        P(None, None, "gx", "gy", "gz", None),
    )
    return jax.shard_map(
        lambda *args: on_device(sizes, *args),
        mesh=mesh,
        in_specs=placed,
        out_specs=(P(None, "gx", "gy", "gz", None), P()),
        check_vma=False,
    )
```

time: 64 us -> 54.8 us (0.86)
  Pallas kernels: 59 us -> 51.5 us
  local copies, waits for them, and re-layouts: 2.6 us -> 1.31 us
    pallas_call x1, Pallas kernels: 59 us -> 51.5 us  [on_device(): pl.pallas_call(lambda *refs: kernel(sizes, *refs), out_shape=(jax.ShapeDt...]
    unnamed x5 -> x3, local copies, waits for them, and re-layouts: 2 us -> 1.31 us
where the time goes in v2:
time: 54.8 us; the launch traced here: 54.6 us
  Pallas kernels  51.5 us (94%)
  between operations  1.81 us (3%)
  local copies, waits for them, and re-layouts  1.31 us (2%)
    pallas_call x1, Pallas kernels, on_device(): pl.pallas_call(lambda *refs: kernel(sizes, *refs), out_shape=(jax.ShapeDt...  51.5 us
    unnamed x3, local copies, waits for them, and re-layouts  1.31 us

profile of v2, /device:TPU:1, one launch (start us, length us, event | category | flops | bytes accessed | tf_op | source)
XLA Modules:
  0.0 54.6 jit_solution(8888406134894127927)
XLA Ops:
  0.6 51.5 %shard_map.77 = (f32[24,128]{1,0:T(8,128)}, f32[1,128]{1,0:T(1,128)}) custom-call(f32[3,4,128]{2,1,0:T(4,128)} %bitcast.14, f32[4,128]{1,0:T(4,128)} %bitcast.15, s32[4,128]{1,0:T(4,128)} %bitcast.16, s32[4,27]{1,0:T(4,128)} %bitcast.17, f32[24,128]{1,0:T(8,128)} %bitcast.12, f32[6,24,128]{2,1,0:T(8,128)} %bitcast.11), custom_call_target="tpu_custom_call" | custom-call | tf_op jit(solution)/shard_map/pallas_call | solution.py:573
  52.1 0.0 copy-start
  52.1 1.3 %copy.11 = f32[6,1,2,2,128]{4,3,2,1,0:T(2,128)} copy(f32[6,1,2,2,128]{4,3,2,1,0:T(2,128)} %bitcast.13) | data formatting | bytes 24576
  53.4 0.0 copy-done
Async XLA Ops:
  52.1 1.3 %copy-start = (f32[1,128]{1,0:T(1,128)S(1)}, f32[1,128]{1,0:T(1,128)}, u32[]{:S(2)}) copy-start(f32[1,128]{1,0:T(1,128)} %get-tuple-element.5) | copy-start | bytes 1540

commit v3 on v2

--- a/solution.py
+++ b/solution.py
@@ -8,7 +8,7 @@
 from jax.sharding import PartitionSpec as P
 
 AXES = ("gx", "gy", "gz")
-FIRST_GROUPS = (("gx",), ("gz",), ("gy",))
+FIRST_GROUPS = (("gy",), ("gz",), ("gx",))
 LAST_GROUPS = (("gx",), ("gy", "gz"))
 MESH = pl.DeviceIdType.MESH
 F32 = jnp.float32
@@ -31,7 +31,7 @@
 
 
 SEMS = 8 + len(FIRST_GROUPS) + len(LAST_GROUPS)
-VMEM_BYTES = 62 * 1000 * 1000
+VMEM_BYTES = 40 * 1024 * 1024
 
 
 def away(sizes, axis, step):
@@ -191,9 +191,14 @@
         load.start()
 
     barrier = pltpu.get_barrier_semaphore()
-    greeted = [neighbour(sizes, direction) for direction in DIRECTIONS]
-    for axis in AXES:
-        greeted += [{axis: away(sizes, axis, step)} for step in range(2, sizes[axis] - 1)]
+    greeted = []
+    for axis in ("gz", "gx", "gy"):
+        greeted += [
+            {axis: away(sizes, axis, step)}
+            for (step,) in group_steps(sizes, (axis,))
+            if 2 <= step <= sizes[axis] - 2
+        ]
+    greeted += [neighbour(sizes, direction) for direction in DIRECTIONS]
     for device in greeted:
         pl.semaphore_signal(barrier, inc=1, device_id=device, device_id_type=MESH)
 
@@ -331,6 +336,9 @@
     for batch in geo_batches + past_batches:
         batch.start()
 
+    row = total(lines_one, 0, line_a)
+    line_b = send_group(FIRST_GROUPS, 1, lines_one, 8, row)
+
     row128 = lax.broadcasted_iota(jnp.int32, (LANES, LANES), 0)
 
     def place_slab(sx):
@@ -350,9 +358,6 @@
 
     lax.fori_loop(0, 8, rim_block, 0)
 
-    row = total(lines_one, 0, line_a)
-    line_b = send_group(FIRST_GROUPS, 1, lines_one, 8, row)
-
     geo_batches[1].arrived()
     place_slab(0)
     place_slab(2)
@@ -363,10 +368,10 @@
         pair_factors(columns[sx, pl.ds(first, 16), :], all_places, "side", sx, first)
         return carry
 
-    lax.fori_loop(0, 11, side_block, 0)
+    lax.fori_loop(0, 4, side_block, 0)
     row = total(lines_one, 1, line_b)
     line_c = send_group(FIRST_GROUPS, 2, lines_one, 8, row)
-    lax.fori_loop(11, 16, side_block, 0)
+    lax.fori_loop(4, 16, side_block, 0)
     row = total(lines_one, 2, line_c)
 
     def entry(a, b):
@@ -449,6 +454,12 @@
     lax.fori_loop(0, 3, predict, 0)
 
     def dot_part(tile, sources):
+        if len(sources) > 6:
+            middle = len(sources) // 2
+            return dot_piece(tile, sources[:middle]) + dot_piece(tile, sources[middle:])
+        return dot_piece(tile, sources)
+
+    def dot_piece(tile, sources):
         ry, rz = RECEIVERS[tile]
         lhs = jnp.concatenate([feats[sx, 4 * sy + sz] for sx, sy, sz in sources], axis=1)
         rhs = jnp.concatenate(
@@ -479,9 +490,13 @@
         return (1.0 - RELAXATION) * before + scaled_tiles[tile] * (perm_tiles[tile] + field)
 
     tile_batches = []
+    summed = dot_part(0, sources_of(0))
     for tile, (ry, rz) in enumerate(RECEIVERS):
+        now = summed
+        if tile < 3:
+            summed = dot_part(tile + 1, sources_of(tile + 1))
         before = moved_one[1, 1 + ry, 1 + rz]
-        moved_two[1, 1 + ry, 1 + rz] = relaxed(tile, before, dot_part(tile, sources_of(tile)))
+        moved_two[1, 1 + ry, 1 + rz] = relaxed(tile, before, now)
         tile_batches.append(tile_batch(sizes, moved_two, sems[4 + tile], tile, counted))
         tile_batches[-1].start()
 
@@ -533,6 +548,10 @@
 
     for batch in ending:
         batch.sent()
+
+
+def in_hbm(array):
+    return pltpu.with_memory_space_constraint(array, pltpu.HBM)
 
 
 def on_device(sizes, fractions, polarizability, occupancy, pair_mask, perm_field, history):
@@ -583,12 +602,12 @@
             collective_id=0, has_side_effects=True, vmem_limit_bytes=VMEM_BYTES
         ),
     )(
-        fractions.reshape(3, 4, LANES),
-        polarizability.reshape(4, LANES),
-        occupancy.reshape(4, LANES),
-        pair_mask.reshape(4, 27),
-        perm_field.reshape(24, LANES),
-        history.reshape(6, 24, LANES),
+        in_hbm(fractions.reshape(3, 4, LANES)),
+        in_hbm(polarizability.reshape(4, LANES)),
+        in_hbm(occupancy.reshape(4, LANES)),
+        in_hbm(pair_mask.reshape(4, 27)),
+        in_hbm(perm_field.reshape(24, LANES)),
+        in_hbm(history.reshape(6, 24, LANES)),
     )
     return induced.reshape(6, 1, 2, 2, LANES), change[0, 0]
 

time: 54.8 us -> 51.4 us (0.938)
  Pallas kernels: 51.5 us -> 48.8 us
  local copies, waits for them, and re-layouts: 1.31 us -> 0.6 us
    pallas_call x1, Pallas kernels: 51.5 us -> 48.8 us  [on_device(): pl.pallas_call(lambda *refs: kernel(sizes, *refs), out_shape=(jax.ShapeDt...]
    unnamed x3 -> x1, local copies, waits for them, and re-layouts: 1.31 us -> 0.6 us
where the time goes in v3:
time: 51.4 us; the launch traced here: 51.2 us
  Pallas kernels  48.8 us (95%)
  between operations  1.8 us (4%)
  local copies, waits for them, and re-layouts  0.6 us (1%)
    pallas_call x1, Pallas kernels, on_device(): pl.pallas_call(lambda *refs: kernel(sizes, *refs), out_shape=(jax.ShapeDt...  48.8 us

profile of v3, /device:TPU:1, one launch (start us, length us, event | category | flops | bytes accessed | tf_op | source)
XLA Modules:
  0.0 51.2 jit_solution(12585630258846540397)
XLA Ops:
  0.6 48.8 %shard_map.77 = (f32[24,128]{1,0:T(8,128)S(1)}, f32[1,128]{1,0:T(1,128)S(1)}) custom-call(f32[3,4,128]{2,1,0:T(4,128)} %bitcast.15, f32[4,128]{1,0:T(4,128)} %bitcast.16, s32[4,128]{1,0:T(4,128)} %bitcast.17, s32[4,27]{1,0:T(4,128)} %bitcast.18, f32[24,128]{1,0:T(8,128)} %bitcast.14, f32[6,24,128]{2,1,0:T(8,128)} %bitcast.13), custom_call_target="tpu_custom_call" | custom-call | tf_op jit(solution)/shard_map/pallas_call | solution.py:592
  49.5 0.6 %copy.11 = f32[6,1,2,2,128]{4,3,2,1,0:T(2,128)} copy(f32[6,1,2,2,128]{4,3,2,1,0:T(2,128)S(1)} %bitcast.11) | data formatting | bytes 24576

commit v4 on v3

--- a/solution.py
+++ b/solution.py
@@ -8,7 +8,7 @@
 from jax.sharding import PartitionSpec as P
 
 AXES = ("gx", "gy", "gz")
-FIRST_GROUPS = (("gy",), ("gz",), ("gx",))
+FIRST_GROUPS = (("gy",), ("gx",), ("gz",))
 LAST_GROUPS = (("gx",), ("gy", "gz"))
 MESH = pl.DeviceIdType.MESH
 F32 = jnp.float32
@@ -159,6 +159,7 @@
     perm_tiles,
     scaled_tiles,
     receiver,
+    own_ends,
     ends,
     own_columns,
     columns,
@@ -226,29 +227,39 @@
         at = (slab + shift) * CELL_EDGE
         return kind == 3, at, DAMP_ROOT * lax.rsqrt(slab)
 
+    def squared(ref, first):
+        parts = [ref[pl.ds(first + n, 1), :] for n in range(3)]
+        return parts[0] * parts[0] + parts[1] * parts[1] + parts[2] * parts[2]
+
     row32 = lax.broadcasted_iota(jnp.int32, (32, LANES), 0)
     last, at, root = positions(
         own_geo[...].reshape(32, LANES), row32, 1, 1 + row32 // 16, 1 + lax.rem(row32 // 8, 2)
     )
-    receiver[...] = jnp.where(last, -root, at)
+    receiver[...] = jnp.where(last, -root, 2.0 * at)
+    own_ends[...] = jnp.where(last, root, at)
+    for tile in range(4):
+        square = squared(own_ends, 8 * tile)
+        receiver[pl.ds(8 * tile + 4, 1)] = square + SOFTENING
+        own_ends[pl.ds(8 * tile + 4, 1)] = square
     own_columns[...] = jnp.transpose(
-        jnp.concatenate([jnp.where(last, root, at), jnp.zeros((96, LANES), F32)], axis=0)
+        jnp.concatenate([own_ends[...], jnp.zeros((96, LANES), F32)], axis=0)
     )
 
     def pair_factors(cols, places, offset_of, sx, first):
         for at, sy, sz in places:
             source = [
-                jnp.broadcast_to(cols[:, at + n : at + n + 1], (16, LANES)) for n in range(4)
+                jnp.broadcast_to(cols[:, at + n : at + n + 1], (16, LANES)) for n in range(5)
             ]
             for tile, (ry, rz) in enumerate(RECEIVERS):
                 ky, kz = sy - ry, sz - rz
                 if not (0 <= ky <= 2 and 0 <= kz <= 2):
                     continue
-                d = [source[n] - receiver[pl.ds(8 * tile + n, 1), :] for n in range(3)]
                 damp = source[3] * receiver[pl.ds(8 * tile + 3, 1), :]
+                dist = source[4] + receiver[pl.ds(8 * tile + 4, 1), :]
+                for n in range(3):
+                    dist = dist - source[n] * receiver[pl.ds(8 * tile + n, 1), :]
                 offset = 9 * sx + 3 * ky + kz
                 allowed = 3.0 * mask_ref[tile, offset].astype(F32)
-                dist = d[0] * d[0] + d[1] * d[1] + d[2] * d[2] + SOFTENING
                 root = lax.rsqrt(dist)
                 inverse = root * root
                 cube = root * inverse * allowed
@@ -279,13 +290,64 @@
             value = jnp.sum(jnp.sum(folded, axis=0, keepdims=True), axis=1, keepdims=True)
             row = jnp.where(lane == 6 * a + b, value, row)
 
+    own_places = [(8 * tile, 1 + ry, 1 + rz) for tile, (ry, rz) in enumerate(RECEIVERS)]
+    all_places = [(8 * (4 * sy + sz), sy, sz) for sy in range(4) for sz in range(4)]
+    rim_places = [(at, sy, sz) for at, sy, sz in all_places if sy in (0, 3) or sz in (0, 3)]
+
+    def own_block(block, carry):
+        for part in range(4):
+            first = pl.multiple_of(block * 64 + part * 16, 16)
+            pair_factors(own_columns[pl.ds(first, 16), :], own_places, "own", 1, first)
+        return carry
+
+    def clear(number, carry):
+        sx, s = number // 16, lax.rem(number, 16)
+        for piece in range(3):
+            feats[sx, s, pl.ds(32 * piece, 16), pl.ds(128, 128)] = jnp.zeros((16, LANES), BF16)
+        return carry
+
+    def send_group(groups, number, bufs, first_sem, values):
+        me, batch = group_batch(sizes, groups[number], bufs[number], sems[first_sem + number])
+        bufs[number][me] = values
+        batch.start()
+        return batch
+
+    def total(bufs, number, batch):
+        batch.arrived()
+        return jnp.sum(bufs[number][...], axis=0)
+
+    pl.semaphore_wait(barrier, len(greeted))
+
+    geo_batches = [halo_batch(sizes, geo, sems[n], n == 0) for n in range(2)]
+    past_batches = [
+        halo_batch(sizes, past, sems[2], True),
+        Batch(
+            [
+                remote(past.at[1], past.at[1 - dx], sems[3], neighbour(sizes, (dx, 0, 0)))
+                for dx in (-1, 1)
+            ],
+            past.at[pl.ds(0, 2)],
+            sems[3],
+            neighbour(sizes, (1, 0, 0)),
+        ),
+    ]
+    line_a = send_group(FIRST_GROUPS, 0, lines_one, 8, row)
+    for batch in geo_batches:
+        batch.start()
+
+    loads[4].wait()
+    lax.fori_loop(0, 2, own_block, 0)
     for tile, (ry, rz) in enumerate(RECEIVERS):
         own = (1, 1 + ry, 1 + rz)
         for h in range(5):
             past[own + (pl.ds(6 * h, 6),)] = masked[h + 1, pl.ds(tile, 6, stride=4), :]
         past[own + (pl.ds(30, 2),)] = jnp.zeros((2, LANES), F32)
 
-    loads[4].wait()
+    row = total(lines_one, 0, line_a)
+    line_b = send_group(FIRST_GROUPS, 1, lines_one, 8, row)
+    past_batches[0].start()
+
+    lax.fori_loop(0, 48, clear, 0, unroll=4)
     loads[5].wait()
     for tile in range(4):
         weight = jnp.broadcast_to(
@@ -299,46 +361,6 @@
                 pl.ds(12 * which + tile, 3, stride=4), :
             ]
 
-    own_places = [(8 * tile, 1 + ry, 1 + rz) for tile, (ry, rz) in enumerate(RECEIVERS)]
-    all_places = [(8 * (4 * sy + sz), sy, sz) for sy in range(4) for sz in range(4)]
-    rim_places = [(at, sy, sz) for at, sy, sz in all_places if sy in (0, 3) or sz in (0, 3)]
-
-    def own_block(block, carry):
-        first = pl.multiple_of(block * 16, 16)
-        pair_factors(own_columns[pl.ds(first, 16), :], own_places, "own", 1, first)
-        return carry
-
-    lax.fori_loop(0, 8, own_block, 0)
-
-    def clear(number, carry):
-        sx, s = number // 16, lax.rem(number, 16)
-        for piece in range(3):
-            feats[sx, s, pl.ds(32 * piece, 16), pl.ds(128, 128)] = jnp.zeros((16, LANES), BF16)
-        return carry
-
-    lax.fori_loop(0, 48, clear, 0, unroll=4)
-
-    def send_group(groups, number, bufs, first_sem, values):
-        me, batch = group_batch(sizes, groups[number], bufs[number], sems[first_sem + number])
-        bufs[number][me] = values
-        batch.start()
-        return batch
-
-    def total(bufs, number, batch):
-        batch.arrived()
-        return jnp.sum(bufs[number][...], axis=0)
-
-    pl.semaphore_wait(barrier, len(greeted))
-
-    geo_batches = [halo_batch(sizes, geo, sems[n], n == 0) for n in range(2)]
-    past_batches = [halo_batch(sizes, past, sems[2 + n], n == 0) for n in range(2)]
-    line_a = send_group(FIRST_GROUPS, 0, lines_one, 8, row)
-    for batch in geo_batches + past_batches:
-        batch.start()
-
-    row = total(lines_one, 0, line_a)
-    line_b = send_group(FIRST_GROUPS, 1, lines_one, 8, row)
-
     row128 = lax.broadcasted_iota(jnp.int32, (LANES, LANES), 0)
 
     def place_slab(sx):
@@ -346,32 +368,44 @@
             geo[sx].reshape(LANES, LANES), row128, sx, row128 // 32, lax.rem(row128 // 8, 4)
         )
         ends[sx] = jnp.where(last, 1.0, at)
-        columns[sx] = jnp.transpose(jnp.where(last, root, at))
+        lengths = at * at
+        lengths = (
+            lengths
+            + pltpu.roll(lengths, LANES - 1, 0)
+            + pltpu.roll(lengths, LANES - 2, 0)
+        )
+        columns[sx] = jnp.transpose(
+            jnp.where(lax.rem(row128, 8) == 4, lengths, jnp.where(last, root, at))
+        )
 
     geo_batches[0].arrived()
     place_slab(1)
 
     def rim_block(block, carry):
-        first = pl.multiple_of(block * 16, 16)
-        pair_factors(columns[1, pl.ds(first, 16), :], rim_places, "rim", 1, first)
+        for part in range(4):
+            first = pl.multiple_of(block * 64 + part * 16, 16)
+            pair_factors(columns[1, pl.ds(first, 16), :], rim_places, "rim", 1, first)
         return carry
 
-    lax.fori_loop(0, 8, rim_block, 0)
-
+    lax.fori_loop(0, 2, rim_block, 0)
+
+    past_batches[0].arrived()
+    past_batches[1].start()
     geo_batches[1].arrived()
     place_slab(0)
     place_slab(2)
 
     def side_block(step, carry):
-        sx = 2 * (step // 8)
-        first = pl.multiple_of(lax.rem(step, 8) * 16, 16)
-        pair_factors(columns[sx, pl.ds(first, 16), :], all_places, "side", sx, first)
+        sx = 2 * (step // 4)
+        for part in range(2):
+            first = pl.multiple_of(lax.rem(step, 4) * 32 + part * 16, 16)
+            pair_factors(columns[sx, pl.ds(first, 16), :], all_places, "side", sx, first)
         return carry
 
-    lax.fori_loop(0, 4, side_block, 0)
+    lax.fori_loop(0, 3, side_block, 0)
     row = total(lines_one, 1, line_b)
     line_c = send_group(FIRST_GROUPS, 2, lines_one, 8, row)
-    lax.fori_loop(4, 16, side_block, 0)
+    lax.fori_loop(3, 8, side_block, 0)
     row = total(lines_one, 2, line_c)
 
     def entry(a, b):
@@ -407,7 +441,6 @@
         coeffs[a] = value * scale[a]
     coeffs = [jnp.broadcast_to(value, (8, LANES))[0:6] for value in coeffs]
 
-    past_batches[0].arrived()
     past_batches[1].arrived()
 
     first_set = sub < 4
@@ -459,13 +492,17 @@
             return dot_piece(tile, sources[:middle]) + dot_piece(tile, sources[middle:])
         return dot_piece(tile, sources)
 
+    def joined(summed):
+        both = summed[:, 0:128] + summed[:, 128:256]
+        return both[0:32] + both[32:64] + both[64:96]
+
     def dot_piece(tile, sources):
         ry, rz = RECEIVERS[tile]
         lhs = jnp.concatenate([feats[sx, 4 * sy + sz] for sx, sy, sz in sources], axis=1)
         rhs = jnp.concatenate(
             [pairs[tile, 9 * sx + 3 * (sy - ry) + sz - rz] for sx, sy, sz in sources], axis=0
         )
-        return jnp.dot(lhs, rhs, preferred_element_type=F32)
+        return joined(jnp.dot(lhs, rhs, preferred_element_type=F32))
 
     def sources_of(tile, kinds=None):
         ry, rz = RECEIVERS[tile]
@@ -477,9 +514,7 @@
             if kinds is None or ((ry + ky + 1) % 2, (rz + kz + 1) % 2) == kinds
         ]
 
-    def relaxed(tile, before, summed):
-        both = summed[:, 0:128] + summed[:, 128:256]
-        out = both[0:32] + both[32:64] + both[64:96]
+    def relaxed(tile, before, out):
         ry, rz = RECEIVERS[tile]
         here = ends[1, pl.ds(8 * (4 * (ry + 1) + rz + 1), 8), :]
         value = out[24:32]
@@ -578,12 +613,13 @@
         pltpu.VMEM((4, 8, LANES), F32),
         pltpu.VMEM((4, 8, LANES), F32),
         pltpu.VMEM((32, LANES), F32),
+        pltpu.VMEM((32, LANES), F32),
         pltpu.VMEM((3, LANES, LANES), F32),
         pltpu.VMEM((LANES, LANES), F32),
         pltpu.VMEM((3, LANES, LANES), F32),
         pltpu.VMEM((4, 27, 256, 256), BF16),
         pltpu.VMEM((3, 16, 96, 256), BF16),
-        pltpu.VMEM((4, 96, 256), F32),
+        pltpu.VMEM((4, 32, LANES), F32),
         pltpu.VMEM((11, 8, LANES), F32),
         dma((6,)),
         dma((SEMS,)),

time: 51.4 us -> 52.3 us (1.018)
  Pallas kernels: 48.8 us -> 49.7 us
    pallas_call x1, Pallas kernels: 48.8 us -> 49.7 us  [on_device(): pl.pallas_call(lambda *refs: kernel(sizes, *refs), out_shape=(jax.ShapeDt...]
where the time goes in v4:
time: 52.3 us; the launch traced here: 52.1 us
  Pallas kernels  49.7 us (95%)
  between operations  1.8 us (3%)
  local copies, waits for them, and re-layouts  0.6 us (1%)
    pallas_call x1, Pallas kernels, on_device(): pl.pallas_call(lambda *refs: kernel(sizes, *refs), out_shape=(jax.ShapeDt...  49.7 us

profile of v4, /device:TPU:1, one launch (start us, length us, event | category | flops | bytes accessed | tf_op | source)
XLA Modules:
  0.0 52.1 jit_solution(17647098760010563567)
XLA Ops:
  0.6 49.7 %shard_map.77 = (f32[24,128]{1,0:T(8,128)S(1)}, f32[1,128]{1,0:T(1,128)S(1)}) custom-call(f32[3,4,128]{2,1,0:T(4,128)} %bitcast.15, f32[4,128]{1,0:T(4,128)} %bitcast.16, s32[4,128]{1,0:T(4,128)} %bitcast.17, s32[4,27]{1,0:T(4,128)} %bitcast.18, f32[24,128]{1,0:T(8,128)} %bitcast.14, f32[6,24,128]{2,1,0:T(8,128)} %bitcast.13), custom_call_target="tpu_custom_call" | custom-call | tf_op jit(solution)/shard_map/pallas_call | solution.py:628
  50.3 0.6 %copy.11 = f32[6,1,2,2,128]{4,3,2,1,0:T(2,128)} copy(f32[6,1,2,2,128]{4,3,2,1,0:T(2,128)S(1)} %bitcast.11) | data formatting | bytes 24576

commit v5 on v4

--- a/solution.py
+++ b/solution.py
@@ -290,6 +290,12 @@
             value = jnp.sum(jnp.sum(folded, axis=0, keepdims=True), axis=1, keepdims=True)
             row = jnp.where(lane == 6 * a + b, value, row)
 
+    for tile, (ry, rz) in enumerate(RECEIVERS):
+        own = (1, 1 + ry, 1 + rz)
+        for h in range(5):
+            past[own + (pl.ds(6 * h, 6),)] = masked[h + 1, pl.ds(tile, 6, stride=4), :]
+        past[own + (pl.ds(30, 2),)] = jnp.zeros((2, LANES), F32)
+
     own_places = [(8 * tile, 1 + ry, 1 + rz) for tile, (ry, rz) in enumerate(RECEIVERS)]
     all_places = [(8 * (4 * sy + sz), sy, sz) for sy in range(4) for sz in range(4)]
     rim_places = [(at, sy, sz) for at, sy, sz in all_places if sy in (0, 3) or sz in (0, 3)]
@@ -334,18 +340,13 @@
     line_a = send_group(FIRST_GROUPS, 0, lines_one, 8, row)
     for batch in geo_batches:
         batch.start()
+    past_batches[0].start()
 
     loads[4].wait()
     lax.fori_loop(0, 2, own_block, 0)
-    for tile, (ry, rz) in enumerate(RECEIVERS):
-        own = (1, 1 + ry, 1 + rz)
-        for h in range(5):
-            past[own + (pl.ds(6 * h, 6),)] = masked[h + 1, pl.ds(tile, 6, stride=4), :]
-        past[own + (pl.ds(30, 2),)] = jnp.zeros((2, LANES), F32)
 
     row = total(lines_one, 0, line_a)
     line_b = send_group(FIRST_GROUPS, 1, lines_one, 8, row)
-    past_batches[0].start()
 
     lax.fori_loop(0, 48, clear, 0, unroll=4)
     loads[5].wait()
@@ -396,16 +397,16 @@
     place_slab(2)
 
     def side_block(step, carry):
-        sx = 2 * (step // 4)
-        for part in range(2):
-            first = pl.multiple_of(lax.rem(step, 4) * 32 + part * 16, 16)
+        sx = 2 * (step // 2)
+        for part in range(4):
+            first = pl.multiple_of(lax.rem(step, 2) * 64 + part * 16, 16)
             pair_factors(columns[sx, pl.ds(first, 16), :], all_places, "side", sx, first)
         return carry
 
-    lax.fori_loop(0, 3, side_block, 0)
+    lax.fori_loop(0, 1, side_block, 0)
     row = total(lines_one, 1, line_b)
     line_c = send_group(FIRST_GROUPS, 2, lines_one, 8, row)
-    lax.fori_loop(3, 8, side_block, 0)
+    lax.fori_loop(1, 4, side_block, 0)
     row = total(lines_one, 2, line_c)
 
     def entry(a, b):

time: 52.3 us -> 49.7 us (0.950)
  Pallas kernels: 49.7 us -> 47.1 us
    pallas_call x1, Pallas kernels: 49.7 us -> 47.1 us  [on_device(): pl.pallas_call(lambda *refs: kernel(sizes, *refs), out_shape=(jax.ShapeDt...]
where the time goes in v5:
time: 49.7 us; the launch traced here: 49.5 us
  Pallas kernels  47.1 us (95%)
  between operations  1.8 us (4%)
  local copies, waits for them, and re-layouts  0.6 us (1%)
    pallas_call x1, Pallas kernels, on_device(): pl.pallas_call(lambda *refs: kernel(sizes, *refs), out_shape=(jax.ShapeDt...  47.1 us

profile of v5, /device:TPU:1, one launch (start us, length us, event | category | flops | bytes accessed | tf_op | source)
XLA Modules:
  0.0 49.5 jit_solution(13269372791255228791)
XLA Ops:
  0.6 47.1 %shard_map.77 = (f32[24,128]{1,0:T(8,128)S(1)}, f32[1,128]{1,0:T(1,128)S(1)}) custom-call(f32[3,4,128]{2,1,0:T(4,128)} %bitcast.15, f32[4,128]{1,0:T(4,128)} %bitcast.16, s32[4,128]{1,0:T(4,128)} %bitcast.17, s32[4,27]{1,0:T(4,128)} %bitcast.18, f32[24,128]{1,0:T(8,128)} %bitcast.14, f32[6,24,128]{2,1,0:T(8,128)} %bitcast.13), custom_call_target="tpu_custom_call" | custom-call | tf_op jit(solution)/shard_map/pallas_call | solution.py:629
  47.7 0.6 %copy.11 = f32[6,1,2,2,128]{4,3,2,1,0:T(2,128)} copy(f32[6,1,2,2,128]{4,3,2,1,0:T(2,128)S(1)} %bitcast.11) | data formatting | bytes 24576

commit v6 on v5

--- a/solution.py
+++ b/solution.py
@@ -505,15 +505,12 @@
         )
         return joined(jnp.dot(lhs, rhs, preferred_element_type=F32))
 
-    def sources_of(tile, kinds=None):
+    def sources_of(tile, wanted=lambda source: True):
         ry, rz = RECEIVERS[tile]
-        return [
-            (sx, ry + ky, rz + kz)
-            for sx in range(3)
-            for ky in range(3)
-            for kz in range(3)
-            if kinds is None or ((ry + ky + 1) % 2, (rz + kz + 1) % 2) == kinds
+        sources = [
+            (sx, ry + ky, rz + kz) for sx in range(3) for ky in range(3) for kz in range(3)
         ]
+        return [source for source in sources if wanted(source)]
 
     def relaxed(tile, before, out):
         ry, rz = RECEIVERS[tile]
@@ -539,24 +536,32 @@
     for batch in geo_batches + past_batches + [line_a, line_b, line_c]:
         batch.sent()
 
+    own_sources = [(1, 1 + ry, 1 + rz) for ry, rz in RECEIVERS]
+
+    def kind_of(source):
+        return 2 * ((source[1] + 1) % 2) + (source[2] + 1) % 2
+
+    for sx, sy, sz in own_sources:
+        write_feats(sx, 4 * sy + sz, moved_two.at[sx, sy, sz])
+    for tile in range(4):
+        partial[tile] = dot_part(tile, own_sources)
+
     changed = flat
     size = flat
-    for kind, kinds in enumerate(RECEIVERS):
-        tile_batches[kind].arrived()
-        tiles = [
-            (sy, sz)
-            for sy in range(4)
-            for sz in range(4)
-            if ((sy + 1) % 2, (sz + 1) % 2) == kinds
-        ]
-        for sx in range(3):
-            for sy, sz in tiles:
+    for kinds in ((0, 1), (2, 3)):
+        for kind in kinds:
+            tile_batches[kind].arrived()
+
+        def arriving(source):
+            return kind_of(source) in kinds and source not in own_sources
+
+        for source in [(sx, sy, sz) for sx in range(3) for sy in range(4) for sz in range(4)]:
+            if arriving(source):
+                sx, sy, sz = source
                 write_feats(sx, 4 * sy + sz, moved_two.at[sx, sy, sz])
         for tile, (ry, rz) in enumerate(RECEIVERS):
-            summed = dot_part(tile, sources_of(tile, kinds))
-            if kind > 0:
-                summed = summed + partial[tile]
-            if kind < 3:
+            summed = partial[tile] + dot_part(tile, sources_of(tile, arriving))
+            if kinds[-1] < 3:
                 partial[tile] = summed
                 continue
             before = moved_two[1, 1 + ry, 1 + rz]

time: 49.7 us -> 49.6 us (level)
  no operation moved by 1% of the time
where the time goes in v6:
time: 49.6 us; the launch traced here: 49.4 us
  Pallas kernels  47 us (95%)
  between operations  1.8 us (4%)
  local copies, waits for them, and re-layouts  0.6 us (1%)
    pallas_call x1, Pallas kernels, on_device(): pl.pallas_call(lambda *refs: kernel(sizes, *refs), out_shape=(jax.ShapeDt...  47 us

profile of v6, /device:TPU:1, one launch (start us, length us, event | category | flops | bytes accessed | tf_op | source)
XLA Modules:
  0.0 49.4 jit_solution(91586327506178901)
XLA Ops:
  0.6 47.0 %shard_map.77 = (f32[24,128]{1,0:T(8,128)S(1)}, f32[1,128]{1,0:T(1,128)S(1)}) custom-call(f32[3,4,128]{2,1,0:T(4,128)} %bitcast.15, f32[4,128]{1,0:T(4,128)} %bitcast.16, s32[4,128]{1,0:T(4,128)} %bitcast.17, s32[4,27]{1,0:T(4,128)} %bitcast.18, f32[24,128]{1,0:T(8,128)} %bitcast.14, f32[6,24,128]{2,1,0:T(8,128)} %bitcast.13), custom_call_target="tpu_custom_call" | custom-call | tf_op jit(solution)/shard_map/pallas_call | solution.py:634
  47.7 0.6 %copy.11 = f32[6,1,2,2,128]{4,3,2,1,0:T(2,128)} copy(f32[6,1,2,2,128]{4,3,2,1,0:T(2,128)S(1)} %bitcast.11) | data formatting | bytes 24576

commit v7 on v6

--- a/solution.py
+++ b/solution.py
@@ -30,7 +30,7 @@
 RECEIVERS = [(ry, rz) for ry in (0, 1) for rz in (0, 1)]
 
 
-SEMS = 8 + len(FIRST_GROUPS) + len(LAST_GROUPS)
+SEMS = 9 + len(FIRST_GROUPS) + len(LAST_GROUPS)
 VMEM_BYTES = 40 * 1024 * 1024
 
 
@@ -77,22 +77,45 @@
         self.whole.wait_send()
 
 
-def halo_batch(sizes, buf, sems, same_slab):
+def halo_copies(sizes, buf, sems, wanted):
     copies = []
     for direction in DIRECTIONS:
         dx, dy, dz = direction
-        if (dx == 0) != same_slab:
-            continue
-        copies.append(
-            remote(
-                buf.at[pl.ds(1, 1), sent_part(dy), sent_part(dz)],
-                buf.at[pl.ds(1 - dx, 1), landing_part(dy), landing_part(dz)],
-                sems,
-                neighbour(sizes, direction),
+        if wanted(direction):
+            copies.append(
+                remote(
+                    buf.at[pl.ds(1, 1), sent_part(dy), sent_part(dz)],
+                    buf.at[pl.ds(1 - dx, 1), landing_part(dy), landing_part(dz)],
+                    sems,
+                    neighbour(sizes, direction),
+                )
             )
-        )
-    counted = buf.at[1, pl.ds(0, 3)] if same_slab else buf.at[pl.ds(0, 2)]
-    return Batch(copies, counted, sems, neighbour(sizes, (0, 0, 1)))
+    return copies
+
+
+def slab_batch(sizes, buf, sems):
+    copies = halo_copies(sizes, buf, sems, lambda direction: direction[0] == 0)
+    return Batch(copies, buf.at[1, pl.ds(0, 3)], sems, neighbour(sizes, (0, 0, 1)))
+
+
+def chip_batches(sizes, buf, chip_sems, sems, counted):
+    odd = lax.rem(lax.axis_index("gx"), 2)
+    me = lax.axis_index("gx") + sizes["gx"]
+    tiles = (pl.ds(1, 2), pl.ds(1, 2))
+    mine = buf.at[(1,) + tiles]
+    partner = {"gx": lax.rem(me + 1 - 2 * odd, sizes["gx"])}
+    beyond = {"gx": lax.rem(me - 1 + 2 * odd, sizes["gx"])}
+    near = Batch(
+        [remote(mine, buf.at[(2 * odd,) + tiles], chip_sems, partner)],
+        buf.at[0, pl.ds(0, 1)],
+        chip_sems,
+        partner,
+    )
+    copies = [remote(mine, buf.at[(2 - 2 * odd,) + tiles], sems, beyond)]
+    copies += halo_copies(
+        sizes, buf, sems, lambda direction: direction[0] != 0 and any(direction[1:])
+    )
+    return near, Batch(copies, counted, sems, partner)
 
 
 def tile_batch(sizes, buf, sems, tile, counted):
@@ -162,6 +185,7 @@
     own_ends,
     ends,
     own_columns,
+    near_columns,
     columns,
     pairs,
     feats,
@@ -218,10 +242,11 @@
         geo[1, 1 + ry, 1 + rz] = own_geo[tile]
 
     def positions(slab, rows, sx, tile_y, tile_z):
+        sx = jnp.asarray(sx).astype(F32)
         kind = lax.rem(rows, 4)
         shift = jnp.where(
             kind == 0,
-            jnp.float32(sx - 1.5),
+            sx - 1.5,
             jnp.where(kind == 1, (tile_y - 2).astype(F32), (tile_z - 2).astype(F32)),
         )
         at = (slab + shift) * CELL_EDGE
@@ -324,9 +349,10 @@
 
     pl.semaphore_wait(barrier, len(greeted))
 
-    geo_batches = [halo_batch(sizes, geo, sems[n], n == 0) for n in range(2)]
+    near_batch, far_batch = chip_batches(sizes, geo, sems[SEMS - 1], sems[1], counted)
+    geo_batches = [near_batch, slab_batch(sizes, geo, sems[0]), far_batch]
     past_batches = [
-        halo_batch(sizes, past, sems[2], True),
+        slab_batch(sizes, past, sems[2]),
         Batch(
             [
                 remote(past.at[1], past.at[1 - dx], sems[3], neighbour(sizes, (dx, 0, 0)))
@@ -345,6 +371,37 @@
     loads[4].wait()
     lax.fori_loop(0, 2, own_block, 0)
 
+    odd = lax.rem(lax.axis_index("gx"), 2)
+    near_slab, far_slab = 2 - 2 * odd, 2 * odd
+
+    near_batch.arrived()
+    last, at, root = positions(
+        geo[near_slab, pl.ds(1, 2), pl.ds(1, 2)].reshape(32, LANES),
+        row32,
+        near_slab,
+        1 + row32 // 16,
+        1 + lax.rem(row32 // 8, 2),
+    )
+    lengths = at * at
+    lengths = lengths + pltpu.roll(lengths, 31, 0) + pltpu.roll(lengths, 30, 0)
+    near_columns[...] = jnp.transpose(
+        jnp.concatenate(
+            [
+                jnp.where(lax.rem(row32, 8) == 4, lengths, jnp.where(last, root, at)),
+                jnp.zeros((96, LANES), F32),
+            ],
+            axis=0,
+        )
+    )
+
+    def near_block(block, carry):
+        for part in range(4):
+            first = pl.multiple_of(block * 64 + part * 16, 16)
+            pair_factors(near_columns[pl.ds(first, 16), :], own_places, "near", near_slab, first)
+        return carry
+
+    lax.fori_loop(0, 2, near_block, 0)
+
     row = total(lines_one, 0, line_a)
     line_b = send_group(FIRST_GROUPS, 1, lines_one, 8, row)
 
@@ -379,7 +436,7 @@
             jnp.where(lax.rem(row128, 8) == 4, lengths, jnp.where(last, root, at))
         )
 
-    geo_batches[0].arrived()
+    geo_batches[1].arrived()
     place_slab(1)
 
     def rim_block(block, carry):
@@ -392,21 +449,28 @@
 
     past_batches[0].arrived()
     past_batches[1].start()
-    geo_batches[1].arrived()
+    geo_batches[2].arrived()
     place_slab(0)
     place_slab(2)
 
-    def side_block(step, carry):
-        sx = 2 * (step // 2)
+    def near_rim_block(block, carry):
         for part in range(4):
-            first = pl.multiple_of(lax.rem(step, 2) * 64 + part * 16, 16)
-            pair_factors(columns[sx, pl.ds(first, 16), :], all_places, "side", sx, first)
+            first = pl.multiple_of(block * 64 + part * 16, 16)
+            cols = columns[near_slab, pl.ds(first, 16), :]
+            pair_factors(cols, rim_places, "near", near_slab, first)
         return carry
 
-    lax.fori_loop(0, 1, side_block, 0)
+    def far_block(block, carry):
+        for part in range(4):
+            first = pl.multiple_of(block * 64 + part * 16, 16)
+            pair_factors(columns[far_slab, pl.ds(first, 16), :], all_places, "far", far_slab, first)
+        return carry
+
+    lax.fori_loop(0, 1, near_rim_block, 0)
     row = total(lines_one, 1, line_b)
     line_c = send_group(FIRST_GROUPS, 2, lines_one, 8, row)
-    lax.fori_loop(1, 4, side_block, 0)
+    lax.fori_loop(1, 2, near_rim_block, 0)
+    lax.fori_loop(0, 2, far_block, 0)
     row = total(lines_one, 2, line_c)
 
     def entry(a, b):
@@ -530,7 +594,7 @@
             summed = dot_part(tile + 1, sources_of(tile + 1))
         before = moved_one[1, 1 + ry, 1 + rz]
         moved_two[1, 1 + ry, 1 + rz] = relaxed(tile, before, now)
-        tile_batches.append(tile_batch(sizes, moved_two, sems[4 + tile], tile, counted))
+        tile_batches.append(tile_batch(sizes, moved_two, sems[4 + tile], tile, counted.at[pl.ds(0, 11)]))
         tile_batches[-1].start()
 
     for batch in geo_batches + past_batches + [line_a, line_b, line_c]:
@@ -622,11 +686,12 @@
         pltpu.VMEM((32, LANES), F32),
         pltpu.VMEM((3, LANES, LANES), F32),
         pltpu.VMEM((LANES, LANES), F32),
+        pltpu.VMEM((LANES, LANES), F32),
         pltpu.VMEM((3, LANES, LANES), F32),
         pltpu.VMEM((4, 27, 256, 256), BF16),
         pltpu.VMEM((3, 16, 96, 256), BF16),
         pltpu.VMEM((4, 32, LANES), F32),
-        pltpu.VMEM((11, 8, LANES), F32),
+        pltpu.VMEM((28, 8, LANES), F32),
         dma((6,)),
         dma((SEMS,)),
         dma((SEMS,)),

time: 49.6 us -> 49.6 us (level)
  no operation moved by 1% of the time
where the time goes in v7:
time: 49.6 us; the launch traced here: 49.4 us
  Pallas kernels  47 us (95%)
  between operations  1.8 us (4%)
  local copies, waits for them, and re-layouts  0.6 us (1%)
    pallas_call x1, Pallas kernels, on_device(): pl.pallas_call(lambda *refs: kernel(sizes, *refs), out_shape=(jax.ShapeDt...  47 us

profile of v7, /device:TPU:1, one launch (start us, length us, event | category | flops | bytes accessed | tf_op | source)
XLA Modules:
  0.0 49.4 jit_solution(4129920056930421214)
XLA Ops:
  0.6 47.0 %shard_map.77 = (f32[24,128]{1,0:T(8,128)S(1)}, f32[1,128]{1,0:T(1,128)S(1)}) custom-call(f32[3,4,128]{2,1,0:T(4,128)} %bitcast.15, f32[4,128]{1,0:T(4,128)} %bitcast.16, s32[4,128]{1,0:T(4,128)} %bitcast.17, s32[4,27]{1,0:T(4,128)} %bitcast.18, f32[24,128]{1,0:T(8,128)} %bitcast.14, f32[6,24,128]{2,1,0:T(8,128)} %bitcast.13), custom_call_target="tpu_custom_call" | custom-call | tf_op jit(solution)/shard_map/pallas_call | solution.py:699
  47.7 0.6 %copy.11 = f32[6,1,2,2,128]{4,3,2,1,0:T(2,128)} copy(f32[6,1,2,2,128]{4,3,2,1,0:T(2,128)S(1)} %bitcast.11) | data formatting | bytes 24576
